TPU v7x, 512 devices: a whole 4x4x16 slice. The times are simulated.
512 devices in a mesh: seq: 64 (over z, x), tp: 8 (over y, core).
Axes of the slice: x: 4, y: 4, z: 16, core: 2. Of those that a mesh axis runs over, the one named last changes fastest.
Arguments:
- mixer_input: bfloat16 [8192, 4096], P('seq', 'tp'), may hold values from -6 to 6
- gate_input: bfloat16 [8192, 4096], P('seq', 'tp'), may hold values from -6 to 6
- document_ids: int32 [8192], P('seq'), may hold values from 0 to 7, never falling along the last dimension, each value on 1 to 2048 neighbouring positions
- residual: bfloat16 [8192, 2048], P('seq'), may hold values from -6 to 6
- select_weight: bfloat16 [4096, 160], P('tp'), may hold values from -0.09375 to 0.09375
- step_weight: bfloat16 [128, 4096], P(None, 'tp'), may hold values from -0.5 to 0.5
- step_bias: float32 [4096], P('tp'), may hold values from -9 to -2.5
- decay_log: float32 [4096, 16], P('tp'), may hold values from -1.5 to 1.5
- skip_gain: float32 [4096], P('tp'), may hold values from 0.1 to 1.9
- out_weight: bfloat16 [4096, 2048], P('tp', 'seq'), may hold values from -0.09375 to 0.09375
- norm_gain: float32 [2048], replicated, may hold values from 0.1 to 1.9
- project_weight: bfloat16 [2048, 3, 2048], P('seq', None, 'tp'), may hold values from -4 to 4
Outputs:
- attention: bfloat16 [8192, 2048], P('seq', 'tp')
Inputs may be any that keep to these rules, and one draw needn't show every extreme that they name: `document_ids`: ids never fall along the sequence; every document has 1 to 2048 tokens.
All inputs are finite; a program needn't handle non-finite values.
Results may differ from a plain program's by a relative error of at most 0.02.
Values may be sent and summed in bfloat16 or wider, within the bound.
A program may use at most 64 MiB of HBM per device.

v0:
```python
import jax
import jax.numpy as jnp
from jax import lax
from jax.sharding import Mesh
from jax.sharding import PartitionSpec as P

STATE = 16
RANK = 128
HEAD = 128
WINDOW = 2048
SEQ = ("seq_0", "seq_1")


norm_eps = 1e-05
unroll_span = 16


def sent_to_all(x, axis):
    size = lax.axis_size(axis)
    return lax.all_to_all(jnp.broadcast_to(x[None], (size, *x.shape)), axis, 0, 0, tiled=True)


def over_copies(x, axis):
    return sent_to_all(x, axis).sum(axis=0)


def filled_with(x, identity):
    return jax.tree.map(
        lambda part, zero: jnp.zeros_like(part) + jnp.asarray(zero, part.dtype), x, identity
    )


def prefix_by_axis(x, axes, combine, identity):
    before = start = filled_with(x, identity)
    running = x
    for axis in reversed(axes):
        size, here = (lax.axis_size(axis), lax.axis_index(axis))
        pieces = jax.tree.map(lambda part: lax.all_gather(part, axis), running)
        inside, running = (start, start)
        for k in range(size):
            passed = k < here
            running = combine(running, jax.tree.map(lambda part: part[k], pieces))
            inside = jax.tree.map(lambda new, old: jnp.where(passed, new, old), running, inside)
        before = combine(inside, before)
    return before


def gather_turned(arrays, axis, dims):
    turned = [jnp.moveaxis(a, dim, 0) for a, dim in zip(arrays, dims)]
    both = jnp.concatenate([t.reshape(len(t), -1) for t in turned], axis=1)
    result, at, gathered = (lax.all_gather(both, axis, axis=0, tiled=True), 0, [])
    for t, dim in zip(turned, dims):
        section = result[:, at : at + t[0].size].reshape(-1, *t.shape[1:])
        gathered.append(jnp.moveaxis(section, 0, dim))
        at += t[0].size
    return tuple(gathered)


def split_up(x, dim, size):
    before, after = (x.shape[:dim], x.shape[dim + 1 :])
    return jnp.moveaxis(x.reshape(*before, size, -1, *after), dim, 0)


def summed_on_arrival(x, axis, dim):
    size = lax.axis_size(axis)
    pieces = lax.all_to_all(split_up(x, dim, size), axis, 0, 0, tiled=True)
    return jnp.sum(pieces, axis=0)


def in_order(pieces, dim):
    pieces = jnp.moveaxis(pieces, 0, dim)
    lengths = pieces.shape
    return pieces.reshape(*lengths[:dim], lengths[dim] * lengths[dim + 1], *lengths[dim + 2 :])


def gathered_copies(x, axis, dim):
    pieces = sent_to_all(x, axis)
    return in_order(pieces, dim)


def passed_along(block, axis, distance):
    devices = range(lax.axis_size(axis))
    route = [(i - distance, i) for i in devices if i - distance in devices]
    return lax.ppermute(block, axis, route)


def local_scan(initial, step_size, input_coef, output_coef, values, keep_flags, decay_rate):
    token_rows, channels = step_size.shape
    block_count = token_rows // unroll_span
    shaped = (
        step_size.reshape(block_count, unroll_span, channels),
        input_coef.reshape(block_count, unroll_span, -1),
        output_coef.reshape(block_count, unroll_span, -1),
        values.reshape(block_count, unroll_span, channels),
        keep_flags.reshape(block_count, unroll_span),
    )

    def advance(carried, block):
        step_rows, input_rows, output_rows, value_rows, keep_rows = block
        outputs = []
        for offset in range(unroll_span):
            carried = (
                jnp.exp(step_rows[offset][:, None] * decay_rate) * carried * keep_rows[offset]
                + (step_rows[offset] * value_rows[offset])[:, None] * input_rows[offset][None, :]
            )
            outputs.append(jnp.sum(carried * output_rows[offset][None, :], axis=1))
        return (carried, jnp.stack(outputs))

    final_state, outputs = lax.scan(advance, initial, shaped)
    return (final_state, outputs.reshape(token_rows, channels))


def carried_part(carry_in, running_steps, output_coef, reach, decay_rate):
    token_rows, channels = running_steps.shape
    block_rows = min(128, token_rows)
    block_count = token_rows // block_rows

    def one_block(block_index):
        growth = jnp.exp(running_steps[:, :, None] * decay_rate[None])
        return jnp.sum(growth * carry_in[None] * output_coef[:, None, :], axis=2) * reach[:, None]

    pieces = lax.map(one_block, jnp.arange(block_count, dtype=jnp.int32))
    return pieces.reshape(token_rows, channels)


def merge_carry(earlier, later):
    prior_decay, prior_state, prior_first, prior_last, prior_start, prior_anchor, prior_empty = (
        earlier
    )
    after_decay, after_state, after_first, after_last, after_start, after_anchor, after_empty = (
        later
    )
    linked = (after_first == prior_last).astype(jnp.float32)
    joined_decay = prior_decay * after_decay * linked
    joined_state = after_state + linked * after_decay * prior_state
    joined_start = jnp.maximum(
        jnp.maximum(prior_start, after_start),
        jnp.where(linked > 0, -1.0, after_anchor).astype(jnp.float32),
    )
    joined = (
        joined_decay,
        joined_state,
        prior_first,
        after_last,
        joined_start,
        prior_anchor,
        jnp.zeros_like(prior_empty),
    )
    return tuple(
        (
            jnp.where(
                prior_empty > 0, after_part, jnp.where(after_empty > 0, prior_part, joined_part)
            )
            for prior_part, after_part, joined_part in zip(earlier, later, joined)
        )
    )


def scale_rows(stream, norm_gain):
    widened = stream.astype(jnp.float32)
    return (
        widened
        * lax.rsqrt(jnp.mean(widened * widened, axis=-1, keepdims=True) + norm_eps)
        * norm_gain
    ).astype(jnp.bfloat16)


def body(
    mixer_input,
    gate_input,
    document_ids,
    residual,
    select_weight,
    step_weight,
    step_bias,
    decay_log,
    skip_gain,
    out_weight,
    norm_gain,
    project_weight,
):
    token_rows, channels = mixer_input.shape
    seq_index = lax.axis_index(SEQ)
    partial_select = jnp.dot(mixer_input, select_weight, preferred_element_type=jnp.float32)
    selected = over_copies(partial_select, "tp")
    step_low = selected[:, :RANK].astype(jnp.bfloat16)
    input_coef = selected[:, RANK : RANK + STATE]
    output_coef = selected[:, RANK + STATE :]
    step_size = jax.nn.softplus(
        jnp.dot(step_low, step_weight, preferred_element_type=jnp.float32) + step_bias
    )
    decay_rate = -jnp.exp(decay_log)
    values = mixer_input.astype(jnp.float32)
    position = seq_index * token_rows + jnp.arange(token_rows, dtype=jnp.int32)
    same_document = document_ids[1:] == document_ids[:-1]
    inner_flags = jnp.concatenate([jnp.ones((1,), jnp.float32), same_document.astype(jnp.float32)])
    zero_state = jnp.zeros((channels, STATE), jnp.float32)
    carry_end, zero_start = local_scan(
        zero_state, step_size, input_coef, output_coef, values, inner_flags, decay_rate
    )
    running_steps = jnp.cumsum(step_size, axis=0)
    decay_total = jnp.exp(decay_rate * running_steps[-1][:, None]) * jnp.all(same_document).astype(
        jnp.float32
    )
    inner_starts = jnp.where(
        jnp.concatenate([jnp.zeros((1,), bool), jnp.logical_not(same_document)]), position, -1
    )
    first_id = document_ids[0].astype(jnp.float32)
    anchor = (seq_index * token_rows).astype(jnp.float32)
    minus_one = jnp.full((), -1.0, jnp.float32)
    identity = (
        jnp.ones_like(decay_total),
        jnp.zeros_like(carry_end),
        minus_one,
        minus_one,
        minus_one,
        jnp.zeros((), jnp.float32),
        jnp.ones((), jnp.float32),
    )
    prefix = prefix_by_axis(
        (
            decay_total,
            carry_end,
            first_id,
            document_ids[-1].astype(jnp.float32),
            jnp.max(inner_starts).astype(jnp.float32),
            anchor,
            jnp.zeros((), jnp.float32),
        ),
        SEQ,
        merge_carry,
        identity,
    )
    follows = (prefix[6] == 0) & (prefix[3] == first_id)
    carry_in = jnp.where(follows, prefix[1], 0.0)
    keep_flags = jnp.concatenate(
        [follows.astype(jnp.float32)[None], same_document.astype(jnp.float32)]
    )
    reach = jnp.cumprod(keep_flags)
    scanned = zero_start + carried_part(carry_in, running_steps, output_coef, reach, decay_rate)
    start_marks = jnp.where(
        jnp.concatenate([jnp.logical_not(follows)[None], jnp.logical_not(same_document)]),
        position,
        -1,
    )
    prior_start = jnp.maximum(prefix[4], 0.0).astype(jnp.int32)
    document_start = jnp.maximum(lax.cummax(start_marks), prior_start)
    gated = ((scanned + skip_gain * values) * jax.nn.silu(gate_input.astype(jnp.float32))).astype(
        jnp.bfloat16
    )
    out_gathered, project_gathered = gather_turned((out_weight, project_weight), SEQ, (1, 0))
    partial_value = jnp.dot(gated, out_gathered, preferred_element_type=jnp.float32)
    row_share = summed_on_arrival(partial_value, "tp", 0)
    share_rows = row_share.shape[0]
    own_rows = lax.dynamic_slice_in_dim(residual, lax.axis_index("tp") * share_rows, share_rows, 0)
    normed = gathered_copies(
        scale_rows((row_share + own_rows.astype(jnp.float32)).astype(jnp.bfloat16), norm_gain),
        "tp",
        0,
    )
    width_local = project_gathered.shape[2]
    triples = jnp.dot(
        normed,
        project_gathered.reshape(project_gathered.shape[0], 3 * width_local),
        preferred_element_type=jnp.float32,
    )
    triples = triples.astype(jnp.bfloat16).reshape(token_rows, 3, width_local)
    queries = triples[:, 0]
    key_value = triples[:, 1:]
    reach_blocks = WINDOW // token_rows
    blocks = [key_value]
    moving = key_value
    for hop_index in range(reach_blocks):
        moving = passed_along(moving, SEQ, 1)
        blocks.insert(0, moving)
    window_rows = jnp.concatenate(blocks, axis=0)
    head_count = width_local // HEAD
    query_heads = queries.reshape(token_rows, head_count, HEAD)
    key_heads = window_rows[:, 0].reshape(-1, head_count, HEAD)
    value_heads = window_rows[:, 1].reshape(-1, head_count, HEAD)
    scores = jnp.einsum(
        "qhd,khd->hqk", query_heads, key_heads, preferred_element_type=jnp.float32
    ) * HEAD ** (-0.5)
    key_position = (seq_index - reach_blocks) * token_rows + jnp.arange(
        (reach_blocks + 1) * token_rows, dtype=jnp.int32
    )
    allowed = (
        (key_position[None, :] <= position[:, None])
        & (key_position[None, :] > position[:, None] - WINDOW)
        & (key_position[None, :] >= document_start[:, None])
    )
    masked = jnp.where(allowed[None], scores, -jnp.inf)
    row_max = jnp.max(masked, axis=-1, keepdims=True)
    weights = jnp.where(allowed[None], jnp.exp(scores - row_max), 0.0)
    weights = (weights / jnp.sum(weights, axis=-1, keepdims=True)).astype(jnp.bfloat16)
    mixed = jnp.einsum("hqk,khd->qhd", weights, value_heads, preferred_element_type=jnp.float32)
    return mixed.astype(jnp.bfloat16).reshape(token_rows, width_local)


def solution(mesh):
    split = Mesh(mesh.devices.reshape(16, 4, mesh.shape["tp"]), ("seq_0", "seq_1", "tp"))
    placed = (
        P(SEQ, "tp"),
        P(SEQ, "tp"),
        P(SEQ),
        P(SEQ, None),
        P("tp", None),
        P(None, "tp"),
        P("tp"),
        P("tp", None),
        P("tp"),
        P("tp", SEQ),
        P(),
        P(SEQ, None, "tp"),
    )
    return jax.shard_map(body, mesh=split, in_specs=placed, out_specs=P(SEQ, "tp"), check_vma=False)
```

profile of v0, /device:TPU:128, one launch (start us, length us, event | category | flops | bytes accessed | tf_op | source)
XLA Modules:
  0.0 613.3 jit_solution(489170180513376221)
XLA Ops:
  23.1 10.5 %all-reduce.11 = (f32[4]{0:T(128)S(1)}, f32[4]{0:T(128)S(1)}, f32[4]{0:T(128)S(1)}, f32[4]{0:T(128)S(1)}, f32[4]{0:T(128)S(1)}) all-reduce(f32[4]{0:T(128)S(1)} %fusion.120, f32[4]{0:T(128)S(1)} %dynamic-update-slice, f32[4]{0:T(128)S(1)} %convert_dynamic-update-slice_fusion, ...), channel_id=1, replica_groups=mesh['seq_0'=16,'seq_1'=4,'tp'=8] {'seq_1'}, use_global_device_ids=true, to_apply=%add.4 | all-reduce | flops 20 | bytes 160
  67.0 30.5 %all-reduce.10 = (f32[16]{0:T(128)S(1)}, f32[16]{0:T(128)S(1)}, f32[16]{0:T(128)S(1)}, f32[16]{0:T(128)S(1)}, f32[16]{0:T(128)S(1)}) all-reduce(f32[16]{0:T(128)S(1)} %dynamic-update-slice.1, f32[16]{0:T(128)S(1)} %dynamic-update-slice.3, f32[16]{0:T(128)S(1)} %dynamic-update-slice.5, ...), channel_id=1, replica_groups=mesh['seq_0'=16,'seq_1'=4,'tp'=8] {'seq_0'}, use_global_device_ids=true, to_apply=%add.1 | all-reduce | flops 80 | bytes 640
  152.0 12.0 %all-gather.1 = f32[2048,16]{0,1:T(8,128)S(1)} all-gather(f32[512,16]{0,1:T(8,128)S(1)} %get-tuple-element.297), channel_id=3, replica_groups=mesh['seq_0'=16,'seq_1'=4,'tp'=8] {'seq_1'}, dimensions={0}, use_global_device_ids=true | all-gather | bytes 163840 | tf_op jit(solution)/shard_map/all_gather | solution.py:38
  164.1 135.0 %while.4 = (s32[]{:T(128)}, f32[512,16]{0,1:T(8,128)S(1)}, f32[8,16,512]{2,1,0:T(8,128)S(1)}, f32[8,16,512]{2,1,0:T(8,128)S(1)}, f32[512,16]{0,1:T(8,128)S(1)}, ...) while((s32[]{:T(128)}, f32[512,16]{0,1:T(8,128)S(1)}, ...), condition=%wide.region_18.19_spmd.clone, body=%wide.region_1.18_spmd.clone.sunk | while | flops 1261586 | bytes 1285524 | solution.py:109
  165.4 10.0 %multiply_reduce_fusion.22 = (f32[512]{0:T(512)S(1)}, f32[512,16]{0,1:T(8,128)S(1)}, f32[512,16]{0,1:T(8,128)S(1)}, f32[512,16]{0,1:T(8,128)S(1)}, f32[512,16]{0...) fusion(f32[16]{0:T(128)S(1)} %get-tuple-element.564, ...), kind=kLoop, calls=%fused_computation.4.clone.1 | loop fusion | flops 679424 | bytes 396417 | tf_op jit(solution)/shard_map/while/body/eval_jaxpr/reduce_sum | solution.py:106
  182.3 10.0 %multiply_reduce_fusion.22 = (f32[512]{0:T(512)S(1)}, f32[512,16]{0,1:T(8,128)S(1)}, f32[512,16]{0,1:T(8,128)S(1)}, f32[512,16]{0,1:T(8,128)S(1)}, f32[512,16]{0...) fusion(f32[16]{0:T(128)S(1)} %get-tuple-element.564, ...), kind=kLoop, calls=%fused_computation.4.clone.1 | loop fusion | flops 679424 | bytes 396417 | tf_op jit(solution)/shard_map/while/body/eval_jaxpr/reduce_sum | solution.py:106
  199.1 10.0 %multiply_reduce_fusion.22 = (f32[512]{0:T(512)S(1)}, f32[512,16]{0,1:T(8,128)S(1)}, f32[512,16]{0,1:T(8,128)S(1)}, f32[512,16]{0,1:T(8,128)S(1)}, f32[512,16]{0...) fusion(f32[16]{0:T(128)S(1)} %get-tuple-element.564, ...), kind=kLoop, calls=%fused_computation.4.clone.1 | loop fusion | flops 679424 | bytes 396417 | tf_op jit(solution)/shard_map/while/body/eval_jaxpr/reduce_sum | solution.py:106
  216.0 10.0 %multiply_reduce_fusion.22 = (f32[512]{0:T(512)S(1)}, f32[512,16]{0,1:T(8,128)S(1)}, f32[512,16]{0,1:T(8,128)S(1)}, f32[512,16]{0,1:T(8,128)S(1)}, f32[512,16]{0...) fusion(f32[16]{0:T(128)S(1)} %get-tuple-element.564, ...), kind=kLoop, calls=%fused_computation.4.clone.1 | loop fusion | flops 679424 | bytes 396417 | tf_op jit(solution)/shard_map/while/body/eval_jaxpr/reduce_sum | solution.py:106
  232.9 10.0 %multiply_reduce_fusion.22 = (f32[512]{0:T(512)S(1)}, f32[512,16]{0,1:T(8,128)S(1)}, f32[512,16]{0,1:T(8,128)S(1)}, f32[512,16]{0,1:T(8,128)S(1)}, f32[512,16]{0...) fusion(f32[16]{0:T(128)S(1)} %get-tuple-element.564, ...), kind=kLoop, calls=%fused_computation.4.clone.1 | loop fusion | flops 679424 | bytes 396417 | tf_op jit(solution)/shard_map/while/body/eval_jaxpr/reduce_sum | solution.py:106
  249.8 10.0 %multiply_reduce_fusion.22 = (f32[512]{0:T(512)S(1)}, f32[512,16]{0,1:T(8,128)S(1)}, f32[512,16]{0,1:T(8,128)S(1)}, f32[512,16]{0,1:T(8,128)S(1)}, f32[512,16]{0...) fusion(f32[16]{0:T(128)S(1)} %get-tuple-element.564, ...), kind=kLoop, calls=%fused_computation.4.clone.1 | loop fusion | flops 679424 | bytes 396417 | tf_op jit(solution)/shard_map/while/body/eval_jaxpr/reduce_sum | solution.py:106
  266.6 10.0 %multiply_reduce_fusion.22 = (f32[512]{0:T(512)S(1)}, f32[512,16]{0,1:T(8,128)S(1)}, f32[512,16]{0,1:T(8,128)S(1)}, f32[512,16]{0,1:T(8,128)S(1)}, f32[512,16]{0...) fusion(f32[16]{0:T(128)S(1)} %get-tuple-element.564, ...), kind=kLoop, calls=%fused_computation.4.clone.1 | loop fusion | flops 679424 | bytes 396417 | tf_op jit(solution)/shard_map/while/body/eval_jaxpr/reduce_sum | solution.py:106
  283.5 10.0 %multiply_reduce_fusion.22 = (f32[512]{0:T(512)S(1)}, f32[512,16]{0,1:T(8,128)S(1)}, f32[512,16]{0,1:T(8,128)S(1)}, f32[512,16]{0,1:T(8,128)S(1)}, f32[512,16]{0...) fusion(f32[16]{0:T(128)S(1)} %get-tuple-element.564, ...), kind=kLoop, calls=%fused_computation.4.clone.1 | loop fusion | flops 679424 | bytes 396417 | tf_op jit(solution)/shard_map/while/body/eval_jaxpr/reduce_sum | solution.py:106
  299.1 12.0 %all-gather = f32[2048,16]{0,1:T(8,128)S(1)} all-gather(f32[512,16]{0,1:T(8,128)S(1)} %get-tuple-element.75), channel_id=2, replica_groups=mesh['seq_0'=16,'seq_1'=4,'tp'=8] {'seq_1'}, dimensions={0}, use_global_device_ids=true | all-gather | bytes 163840 | tf_op jit(solution)/shard_map/all_gather | solution.py:38
  311.2 30.4 %all_gather.90 = f32[16,512,16]{1,2,0:T(8,128)S(1)} all-gather(f32[1,512,16]{1,2,0:T(8,128)S(1)} %select_select_fusion), channel_id=1, replica_groups=mesh['seq_0'=16,'seq_1'=4,'tp'=8] {'seq_0'}, dimensions={0}, use_global_device_ids=true | all-gather | bytes 557056 | tf_op jit(solution)/shard_map/all_gather | solution.py:38
  341.6 30.6 %all_gather.87 = f32[16,512,16]{1,2,0:T(8,128)S(1)} all-gather(f32[1,512,16]{1,2,0:T(8,128)S(1)} %select_select_fusion.3), channel_id=1, replica_groups=mesh['seq_0'=16,'seq_1'=4,'tp'=8] {'seq_0'}, dimensions={0}, use_global_device_ids=true | all-gather | bytes 557056 | tf_op jit(solution)/shard_map/all_gather | solution.py:38
  382.1 15.9 %all-to-all-done.1 = f32[8,16,2048]{2,1,0:T(8,128)S(1)} async-done(((f32[8,16,2048]{2,1,0:T(8,128)}), f32[8,16,2048]{2,1,0:T(8,128)S(1)}, u32[]{:S(2)}, u32[]{:S(2)}) %all-to-all-start.1) | async-done | bytes 1048608 | tf_op jit(solution)/shard_map/all_to_all | solution.py:66
  399.3 12.8 %all_to_all.15 = bf16[8,16,2048]{2,1,0:T(8,128)(2,1)S(1)} all-to-all(bf16[8,16,2048]{2,1,0:T(8,128)(2,1)S(1)} %broadcast_in_dim.74), channel_id=1, replica_groups=mesh['seq_0'=16,'seq_1'=4,'tp'=8] {'tp'}, dimensions={0} | all-to-all | bytes 1048576 | tf_op jit(solution)/shard_map/all_to_all | solution.py:20
  416.6 8.3 %collective-permute-done = bf16[128,2,256]{0,2,1:T(8,128)(2,1)S(1)} collective-permute-done((bf16[128,2,256]{0,2,1:T(8,128)(2,1)S(1)}, bf16[128,2,256]{0,2,1:T(8,128)(2,1)S(1)}, u32[]{:S(2)}, u32[]{:S(2)}) %collective-permute-start) | collective-permute-done | bytes 131104 | tf_op jit(solution)/shard_map/ppermute | solution.py:84
  426.8 8.3 %collective-permute-done.1 = bf16[128,2,256]{0,2,1:T(8,128)(2,1)S(1)} collective-permute-done((bf16[128,2,256]{0,2,1:T(8,128)(2,1)S(1)}, bf16[128,2,256]{0,2,1:T(8,128)(2,1)S(1)}, u32[]{:S(2)}, u32[]{:S(2)}) %collective-permute-start.1) | collective-permute-done | bytes 131104 | tf_op jit(solution)/shard_map/ppermute | solution.py:84
  437.0 8.3 %collective-permute-done.2 = bf16[128,2,256]{0,2,1:T(8,128)(2,1)S(1)} collective-permute-done((bf16[128,2,256]{0,2,1:T(8,128)(2,1)S(1)}, bf16[128,2,256]{0,2,1:T(8,128)(2,1)S(1)}, u32[]{:S(2)}, u32[]{:S(2)}) %collective-permute-start.2) | collective-permute-done | bytes 131104 | tf_op jit(solution)/shard_map/ppermute | solution.py:84
  447.2 8.3 %collective-permute-done.3 = bf16[128,2,256]{0,2,1:T(8,128)(2,1)S(1)} collective-permute-done((bf16[128,2,256]{0,2,1:T(8,128)(2,1)S(1)}, bf16[128,2,256]{0,2,1:T(8,128)(2,1)S(1)}, u32[]{:S(2)}, u32[]{:S(2)}) %collective-permute-start.3) | collective-permute-done | bytes 131104 | tf_op jit(solution)/shard_map/ppermute | solution.py:84
  477.7 9.0 %collective-permute-done.6 = bf16[128,2,256]{0,2,1:T(8,128)(2,1)S(1)} collective-permute-done((bf16[128,2,256]{0,2,1:T(8,128)(2,1)S(1)}, bf16[128,2,256]{0,2,1:T(8,128)(2,1)S(1)}, u32[]{:S(2)}, u32[]{:S(2)}) %collective-permute-start.6) | collective-permute-done | bytes 131104 | tf_op jit(solution)/shard_map/ppermute | solution.py:84
  488.6 9.1 %collective-permute-done.7 = bf16[128,2,256]{0,2,1:T(8,128)(2,1)S(1)} collective-permute-done((bf16[128,2,256]{0,2,1:T(8,128)(2,1)S(1)}, bf16[128,2,256]{0,2,1:T(8,128)(2,1)S(1)}, u32[]{:S(2)}, u32[]{:S(2)}) %collective-permute-start.7) | collective-permute-done | bytes 131104 | tf_op jit(solution)/shard_map/ppermute | solution.py:84
  499.7 8.3 %collective-permute-done.8 = bf16[128,2,256]{0,2,1:T(8,128)(2,1)S(1)} collective-permute-done((bf16[128,2,256]{0,2,1:T(8,128)(2,1)S(1)}, bf16[128,2,256]{0,2,1:T(8,128)(2,1)S(1)}, u32[]{:S(2)}, u32[]{:S(2)}) %collective-permute-start.8) | collective-permute-done | bytes 131104 | tf_op jit(solution)/shard_map/ppermute | solution.py:84
  (369 shorter events, 194.1 us)
Async XLA Ops:
  6.5 133.5 %copy-start.1 = (bf16[128,512]{1,0:T(8,128)(2,1)S(1)}, bf16[128,512]{1,0:T(8,128)(2,1)}, u32[]{:S(2)}) copy-start(bf16[128,512]{1,0:T(8,128)(2,1)} %param.14) | copy-start | bytes 393220
  9.5 141.8 %copy-start.9 = (bf16[128,512]{1,0:T(8,128)(2,1)S(1)}, bf16[128,512]{1,0:T(8,128)(2,1)}, u32[]{:S(2)}) copy-start(bf16[128,512]{1,0:T(8,128)(2,1)} %param.19) | copy-start | bytes 393220
  9.5 141.8 %copy-start.10 = (f32[512]{0:T(512)S(1)}, f32[512]{0:T(512)}, u32[]{:S(2)}) copy-start(f32[512]{0:T(512)} %param.20) | copy-start | bytes 6148
  9.5 141.6 %all-to-all-start = ((f32[8,128,160]{1,2,0:T(8,128)}), f32[8,128,160]{1,2,0:T(8,128)S(1)}, u32[]{:S(2)}, u32[]{:S(2)}) async-start(f32[8,128,160]{1,2,0:T(8,128)} %broadcast_in_dim.70), calls=%async_computation | async-start | bytes 1310720 | tf_op jit(solution)/shard_map/all_to_all | solution.py:20
  14.1 137.8 %copy-start.5 = (f32[512,16]{0,1:T(8,128)S(1)}, f32[512,16]{0,1:T(8,128)}, u32[]{:S(2)}) copy-start(f32[512,16]{0,1:T(8,128)} %param.21) | copy-start | bytes 98308
  14.1 359.8 %all-gather.4.cloned.1.call-start = ((), (), s32[]{:S(2)}) async-start(), calls=%async_computation.3 | async-start | bytes 5324800 | tf_op jit(solution)/shard_map/all_gather | solution.py:51
  311.1 62.6 %copy-start.2 = (bf16[128,512]{1,0:T(8,128)(2,1)S(1)}, bf16[128,512]{1,0:T(8,128)(2,1)}, u32[]{:S(2)}) copy-start(bf16[128,512]{1,0:T(8,128)(2,1)} %param.15) | copy-start | bytes 393220
  377.3 20.8 %all-to-all-start.1 = ((f32[8,16,2048]{2,1,0:T(8,128)}), f32[8,16,2048]{2,1,0:T(8,128)S(1)}, u32[]{:S(2)}, u32[]{:S(2)}) async-start(f32[8,16,2048]{2,1,0:T(8,128)} %bitcast.83), calls=%async_computation.1 | async-start | bytes 2097152 | tf_op jit(solution)/shard_map/all_to_all | solution.py:66
  414.7 10.2 %collective-permute-start = (bf16[128,2,256]{0,2,1:T(8,128)(2,1)S(1)}, bf16[128,2,256]{0,2,1:T(8,128)(2,1)S(1)}, u32[]{:S(2)}, u32[]{:S(2)}) collective-permute-start(bf16[128,2,256]{0,2,1:T(8,128)(2,1)S(1)} %slice.1077), channel_id=1, source_target_pairs={{0,8},{8,16},{16,24},{24,32},{32,40},{40,48},{48,56},{56,64},{64,7... | collective-permute-start | bytes 393224 | tf_op jit(solution)/shard_map/ppermute | solution.py:84
  424.9 10.2 %collective-permute-start.1 = (bf16[128,2,256]{0,2,1:T(8,128)(2,1)S(1)}, bf16[128,2,256]{0,2,1:T(8,128)(2,1)S(1)}, u32[]{:S(2)}, u32[]{:S(2)}) collective-permute-start(bf16[128,2,256]{0,2,1:T(8,128)(2,1)S(1)} %collective-permute-done), channel_id=1, source_target_pairs={{0,8},{8,16},{16,24},{24,32},{32,40},{40,48},{48,56},{56,64},{64,7... | collective-permute-start | bytes 393224 | tf_op jit(solution)/shard_map/ppermute | solution.py:84
  435.1 10.2 %collective-permute-start.2 = (bf16[128,2,256]{0,2,1:T(8,128)(2,1)S(1)}, bf16[128,2,256]{0,2,1:T(8,128)(2,1)S(1)}, u32[]{:S(2)}, u32[]{:S(2)}) collective-permute-start(bf16[128,2,256]{0,2,1:T(8,128)(2,1)S(1)} %collective-permute-done.1), channel_id=1, source_target_pairs={{0,8},{8,16},{16,24},{24,32},{32,40},{40,48},{48,56},{56,64},{64,7... | collective-permute-start | bytes 393224 | tf_op jit(solution)/shard_map/ppermute | solution.py:84
  445.2 10.2 %collective-permute-start.3 = (bf16[128,2,256]{0,2,1:T(8,128)(2,1)S(1)}, bf16[128,2,256]{0,2,1:T(8,128)(2,1)S(1)}, u32[]{:S(2)}, u32[]{:S(2)}) collective-permute-start(bf16[128,2,256]{0,2,1:T(8,128)(2,1)S(1)} %collective-permute-done.2), channel_id=1, source_target_pairs={{0,8},{8,16},{16,24},{24,32},{32,40},{40,48},{48,56},{56,64},{64,7... | collective-permute-start | bytes 393224 | tf_op jit(solution)/shard_map/ppermute | solution.py:84
  455.4 10.2 %collective-permute-start.4 = (bf16[128,2,256]{0,2,1:T(8,128)(2,1)S(1)}, bf16[128,2,256]{0,2,1:T(8,128)(2,1)S(1)}, u32[]{:S(2)}, u32[]{:S(2)}) collective-permute-start(bf16[128,2,256]{0,2,1:T(8,128)(2,1)S(1)} %collective-permute-done.3), channel_id=1, source_target_pairs={{0,8},{8,16},{16,24},{24,32},{32,40},{40,48},{48,56},{56,64},{64,7... | collective-permute-start | bytes 393224 | tf_op jit(solution)/shard_map/ppermute | solution.py:84
  465.6 10.2 %collective-permute-start.5 = (bf16[128,2,256]{0,2,1:T(8,128)(2,1)S(1)}, bf16[128,2,256]{0,2,1:T(8,128)(2,1)S(1)}, u32[]{:S(2)}, u32[]{:S(2)}) collective-permute-start(bf16[128,2,256]{0,2,1:T(8,128)(2,1)S(1)} %collective-permute-done.4), channel_id=1, source_target_pairs={{0,8},{8,16},{16,24},{24,32},{32,40},{40,48},{48,56},{56,64},{64,7... | collective-permute-start | bytes 393224 | tf_op jit(solution)/shard_map/ppermute | solution.py:84
  475.7 10.9 %collective-permute-start.6 = (bf16[128,2,256]{0,2,1:T(8,128)(2,1)S(1)}, bf16[128,2,256]{0,2,1:T(8,128)(2,1)S(1)}, u32[]{:S(2)}, u32[]{:S(2)}) collective-permute-start(bf16[128,2,256]{0,2,1:T(8,128)(2,1)S(1)} %collective-permute-done.5), channel_id=1, source_target_pairs={{0,8},{8,16},{16,24},{24,32},{32,40},{40,48},{48,56},{56,64},{64,7... | collective-permute-start | bytes 393224 | tf_op jit(solution)/shard_map/ppermute | solution.py:84
  486.7 11.1 %collective-permute-start.7 = (bf16[128,2,256]{0,2,1:T(8,128)(2,1)S(1)}, bf16[128,2,256]{0,2,1:T(8,128)(2,1)S(1)}, u32[]{:S(2)}, u32[]{:S(2)}) collective-permute-start(bf16[128,2,256]{0,2,1:T(8,128)(2,1)S(1)} %collective-permute-done.6), channel_id=1, source_target_pairs={{0,8},{8,16},{16,24},{24,32},{32,40},{40,48},{48,56},{56,64},{64,7... | collective-permute-start | bytes 393224 | tf_op jit(solution)/shard_map/ppermute | solution.py:84
  497.7 10.2 %collective-permute-start.8 = (bf16[128,2,256]{0,2,1:T(8,128)(2,1)S(1)}, bf16[128,2,256]{0,2,1:T(8,128)(2,1)S(1)}, u32[]{:S(2)}, u32[]{:S(2)}) collective-permute-start(bf16[128,2,256]{0,2,1:T(8,128)(2,1)S(1)} %collective-permute-done.7), channel_id=1, source_target_pairs={{0,8},{8,16},{16,24},{24,32},{32,40},{40,48},{48,56},{56,64},{64,7... | collective-permute-start | bytes 393224 | tf_op jit(solution)/shard_map/ppermute | solution.py:84
  507.9 10.2 %collective-permute-start.9 = (bf16[128,2,256]{0,2,1:T(8,128)(2,1)S(1)}, bf16[128,2,256]{0,2,1:T(8,128)(2,1)S(1)}, u32[]{:S(2)}, u32[]{:S(2)}) collective-permute-start(bf16[128,2,256]{0,2,1:T(8,128)(2,1)S(1)} %collective-permute-done.8), channel_id=1, source_target_pairs={{0,8},{8,16},{16,24},{24,32},{32,40},{40,48},{48,56},{56,64},{64,7... | collective-permute-start | bytes 393224 | tf_op jit(solution)/shard_map/ppermute | solution.py:84
  518.1 10.2 %collective-permute-start.10 = (bf16[128,2,256]{0,2,1:T(8,128)(2,1)S(1)}, bf16[128,2,256]{0,2,1:T(8,128)(2,1)S(1)}, u32[]{:S(2)}, u32[]{:S(2)}) collective-permute-start(bf16[128,2,256]{0,2,1:T(8,128)(2,1)S(1)} %collective-permute-done.9), channel_id=1, source_target_pairs={{0,8},{8,16},{16,24},{24,32},{32,40},{40,48},{48,56},{56,64},{64,7... | collective-permute-start | bytes 393224 | tf_op jit(solution)/shard_map/ppermute | solution.py:84
  528.3 10.2 %collective-permute-start.11 = (bf16[128,2,256]{0,2,1:T(8,128)(2,1)S(1)}, bf16[128,2,256]{0,2,1:T(8,128)(2,1)S(1)}, u32[]{:S(2)}, u32[]{:S(2)}) collective-permute-start(bf16[128,2,256]{0,2,1:T(8,128)(2,1)S(1)} %collective-permute-done.10), channel_id=1, source_target_pairs={{0,8},{8,16},{16,24},{24,32},{32,40},{40,48},{48,56},{56,64},{64,7... | collective-permute-start | bytes 393224 | tf_op jit(solution)/shard_map/ppermute | solution.py:84
  538.5 10.2 %collective-permute-start.12 = (bf16[128,2,256]{0,2,1:T(8,128)(2,1)S(1)}, bf16[128,2,256]{0,2,1:T(8,128)(2,1)S(1)}, u32[]{:S(2)}, u32[]{:S(2)}) collective-permute-start(bf16[128,2,256]{0,2,1:T(8,128)(2,1)S(1)} %collective-permute-done.11), channel_id=1, source_target_pairs={{0,8},{8,16},{16,24},{24,32},{32,40},{40,48},{48,56},{56,64},{64,7... | collective-permute-start | bytes 393224 | tf_op jit(solution)/shard_map/ppermute | solution.py:84
  548.6 10.2 %collective-permute-start.13 = (bf16[128,2,256]{0,2,1:T(8,128)(2,1)S(1)}, bf16[128,2,256]{0,2,1:T(8,128)(2,1)S(1)}, u32[]{:S(2)}, u32[]{:S(2)}) collective-permute-start(bf16[128,2,256]{0,2,1:T(8,128)(2,1)S(1)} %collective-permute-done.12), channel_id=1, source_target_pairs={{0,8},{8,16},{16,24},{24,32},{32,40},{40,48},{48,56},{56,64},{64,7... | collective-permute-start | bytes 393224 | tf_op jit(solution)/shard_map/ppermute | solution.py:84
  558.8 34.0 %collective-permute-start.14 = (bf16[128,2,256]{0,2,1:T(8,128)(2,1)S(1)}, bf16[128,2,256]{0,2,1:T(8,128)(2,1)S(1)}, u32[]{:S(2)}, u32[]{:S(2)}) collective-permute-start(bf16[128,2,256]{0,2,1:T(8,128)(2,1)S(1)} %collective-permute-done.13), channel_id=1, source_target_pairs={{0,8},{8,16},{16,24},{24,32},{32,40},{40,48},{48,56},{56,64},{64,7... | collective-permute-start | bytes 393224 | tf_op jit(solution)/shard_map/ppermute | solution.py:84
  592.8 10.2 %collective-permute-start.15 = (bf16[128,2,256]{0,2,1:T(8,128)(2,1)S(1)}, bf16[128,2,256]{0,2,1:T(8,128)(2,1)S(1)}, u32[]{:S(2)}, u32[]{:S(2)}) collective-permute-start(bf16[128,2,256]{0,2,1:T(8,128)(2,1)S(1)} %collective-permute-done.14), channel_id=1, source_target_pairs={{0,8},{8,16},{16,24},{24,32},{32,40},{40,48},{48,56},{56,64},{64,7... | collective-permute-start | bytes 393224 | tf_op jit(solution)/shard_map/ppermute | solution.py:84
  (6 other events, 109.0 us)
Sparse Core Ops, SparseCore 0:
  17.9 148.5 all-gather.3
where the time goes:
time: 618 us; the launch traced here: 613 us
  waiting for transfers between devices  139 us (22%)
  blocking collectives  139 us (22%)
  other arithmetic  134 us (22%)
  between operations  124 us (20%)
  starting transfers between devices  40.2 us (7%)
  local copies, waits for them, and re-layouts  28.2 us (5%)
  matrix products  8.37 us (1%)
    reduce_sum x40, other arithmetic, advance(): outputs.append(jnp.sum(carried * output_rows[offset][None, :], axis=1))  124 us
    ppermute x16, waiting for transfers between devices, passed_along(): return lax.ppermute(block, axis, route)  123 us
    all_gather x4, blocking collectives, prefix_by_axis(): pieces = jax.tree.map(lambda part: lax.all_gather(part, axis), running)  84.9 us
    unnamed x2, blocking collectives  41 us
    ppermute x16, starting transfers between devices, passed_along(): return lax.ppermute(block, axis, route)  30.7 us
    all_to_all x1, waiting for transfers between devices, summed_on_arrival(): pieces = lax.all_to_all(split_up(x, dim, size), axis, 0, 0, tiled=True)  15.9 us
    all_to_all x1, blocking collectives, sent_to_all(): lax.all_to_all(jnp.broadcast_to(x[None], (size, *x.shape)), axis, 0, 0, t...  12.8 us
  transfers between devices with their start and end apart: 19, of which 16 were waited for; matrix products, arithmetic and copies ran while one was open for 26% of the time, Pallas kernels for 0%

commit v1 on v0

v1 whole, which is shorter than its diff:
```python
import jax
import jax.numpy as jnp
from jax import lax
from jax.experimental import pallas as pl
from jax.experimental.pallas import tpu as pltpu
from jax.sharding import Mesh
from jax.sharding import PartitionSpec as P

MESH = pl.DeviceIdType.MESH
NZ, NX, NY, NC = 16, 4, 4, 2
STATE = 16
RANK = 128
HEAD = 128
WINDOW = 2048
EPS = 1e-05
LOG2E = 1.4426950408889634
RESET = 1e6
HIDDEN = -1e30
SEQ = ("z", "x")
TP = ("y", "c")
F32 = jnp.float32
BF16 = jnp.bfloat16


def nt(a, b):
    return lax.dot_general(a, b, (((1,), (1,)), ((), ())), preferred_element_type=F32)


def nn(a, b):
    return jnp.dot(a, b, preferred_element_type=F32)


def iota(shape, dim):
    return lax.broadcasted_iota(jnp.int32, shape, dim)


def softplus(v):
    e = jnp.exp(-jnp.abs(v))
    small = e * (1.0 - e * (0.5 - e * (1.0 / 3.0 - e * 0.25)))
    return jnp.maximum(v, 0.0) + jnp.where(e < 0.01, small, jnp.log(1.0 + e))


class Links:
    def __init__(self, send, recv):
        self.send, self.recv = send, recv
        self.sends, self.recvs = 0, 0
        self.open = []

    def slots(self, count):
        first = self.recvs
        self.recvs += count
        return first

    def copy(self, src, dst, device, slot, send=None):
        if send is None:
            send = self.sends
            self.sends += 1
        return pltpu.make_async_remote_copy(
            src_ref=src,
            dst_ref=dst,
            send_sem=self.send.at[send],
            recv_sem=self.recv.at[slot],
            device_id=device,
            device_id_type=MESH,
        )

    def start(self, src, dst, device, slot):
        made = self.copy(src, dst, device, slot)
        made.start()
        self.open.append(made)

    def wait(self, dst, slot, device):
        self.copy(dst, dst, device, slot, 0).wait_recv()

    def drain(self):
        for made in self.open:
            made.wait_send()


def kernel(
    x_ref, g_ref, ids_ref, res_ref, sel_ref, stepw_ref, bias_ref, a_ref, skip_ref, wo_ref, gain_ref, wp_ref,
    out_ref,
    part, rs1, sb, ids, dt2, bx, hb, hs, ss, hz, sz, hr, sr, xw, wp, ys, gt, ps, pr, ow, r2s, r2, na, nb,
    kv, qd, ob, outb, send_sem, recv_sem,
):
    z, x, y, c = (lax.axis_index(n) for n in ("z", "x", "y", "c"))
    other = 1 - c

    def zat(d):
        return lax.rem(z + d + NZ, NZ)

    def xat(d):
        return lax.rem(x + d, NX)

    def yat(d):
        return lax.rem(y + d, NY)

    def cat(d):
        return other if d else c

    peers = [(z, x, yat(dy), cat(dc)) for dy in range(NY) for dc in range(NC) if dy or dc]
    row_peers = [(z, xat(dx), y, cat(dc)) for dx in range(1, NX) for dc in range(NC)]
    far = [(zat(d), x, y, c) for d in (-4, -3, -2, -1, 1, 2, 3, 4)]
    barrier = pltpu.get_barrier_semaphore()
    everyone = peers + row_peers + far
    for device in everyone:
        pl.semaphore_signal(barrier, inc=1, device_id=device, device_id_type=MESH)

    links = Links(send_sem, recv_sem)
    me = (z, x, y, c)
    partner = (z, x, y, other)
    my_rows = pl.multiple_of(64 * c + 16 * y, 16)

    part[...] = nn(x_ref[...], sel_ref[...])
    xw[z, x] = wo_ref[...]
    ids[0, :, pl.ds(pl.multiple_of(128 * x, 128), 128)] = ids_ref[...]
    pl.semaphore_wait(barrier, len(everyone))

    slot_rs = links.slots(8)
    for dy in range(NY):
        for dc in range(NC):
            if dy or dc:
                ty, tc = yat(dy), cat(dc)
                rows = pl.multiple_of(64 * tc + 16 * ty, 16)
                links.start(part.at[pl.ds(rows, 16)], rs1.at[dy * 2 + dc], (z, x, ty, tc), slot_rs + dy * 2 + dc)

    slot_x0 = links.slots(2)
    for hh in range(2):
        links.start(wp_ref.at[hh], wp.at[z, x], (z, 2 * c + hh, y, 1 - x // 2), slot_x0 + lax.rem(x, 2))
    slot_i1 = links.slots(4)
    row_part = pl.ds(pl.multiple_of(128 * x, 128), 128)
    for dx in range(1, NX):
        links.start(ids_ref, ids.at[0, :, row_part], (z, xat(dx), y, c), slot_i1 + dx)

    slot_wo = {d: links.slots(1) for d in (-7, -6, -5, -4, -3, -2, -1, 1, 2, 3, 4, 5, 6, 7, 8)}
    slot_wp = {d: links.slots(1) for d in (-7, -6, -5, -4, -3, -2, -1, 1, 2, 3, 4, 5, 6, 7, 8)}
    ringed = pl.ds(pl.multiple_of(2 * other, 2), 2)

    def hops(phase):
        right = [2 * phase - 1, 2 * phase]
        left = [-d for d in right if d < 8]
        return right + left

    def ring_out(phase):
        for sign in (1, -1):
            block = zat(-sign * 2 * (phase - 1))
            for near in (1, 2):
                far_by = sign * (2 * (phase - 1) + near)
                if far_by != -8:
                    links.start(
                        wo_ref if phase == 1 else xw.at[block, x],
                        xw.at[block, x],
                        (zat(sign * near), x, y, c),
                        slot_wo[far_by],
                    )

    def ring_proj(phase):
        for sign in (1, -1):
            block = zat(-sign * 2 * (phase - 1))
            for near in (1, 2):
                far_by = sign * (2 * (phase - 1) + near)
                if far_by != -8:
                    links.start(
                        wp.at[block, ringed],
                        wp.at[block, ringed],
                        (zat(sign * near), x, y, c),
                        slot_wp[far_by],
                    )

    def ring_wait(phase, slots, at):
        for d in hops(phase):
            links.wait(at(zat(-d)), slots[d], (zat(1 if d > 0 else -1), x, y, c))

    def wo_at(block):
        return xw.at[block, x]

    def wp_at(block):
        return wp.at[block, ringed]

    slot_xw = links.slots(4)
    first_xw = links.sends
    links.sends += 3

    def spread(blocks):
        for block in blocks:
            for dx in range(1, NX):
                links.copy(
                    xw.at[block, x], xw.at[block, x], (z, xat(dx), y, c), slot_xw + dx, first_xw + dx - 1
                ).start()

    ring_out(1)

    total = part[pl.ds(my_rows, 16), :]
    for k in range(1, 8):
        links.wait(rs1.at[k], slot_rs + k, partner)
        total = total + rs1[k]
    sb[pl.ds(my_rows, 16), :] = total.astype(BF16)
    slot_ag = links.slots(8)
    for dy in range(NY):
        for dc in range(NC):
            if dy or dc:
                mine = sb.at[pl.ds(my_rows, 16)]
                links.start(mine, mine, (z, x, yat(dy), cat(dc)), slot_ag + dy * 2 + dc)

    for dx in range(1, NX):
        links.wait(ids.at[0, :, row_part], slot_i1 + dx, (z, xat(dx), y, c))
    slot_i2 = links.slots(5)
    for dz in range(1, 5):
        links.start(ids.at[0], ids.at[dz], (zat(dz), x, y, c), slot_i2 + dz)
    for k in range(2):
        links.wait(wp.at[z, x], slot_x0 + k, partner)
    ring_proj(1)

    for k in range(1, 8):
        links.wait(sb.at[pl.ds(my_rows, 16)], slot_ag + k, partner)
    for dz in range(1, 5):
        links.wait(ids.at[dz], slot_i2 + dz, (zat(dz), x, y, c))

    values = x_ref[...].astype(F32)
    step = softplus(nn(sb[:, :RANK], stepw_ref[...]) + bias_ref[...])
    last = [jnp.broadcast_to(ids[0, :, 128 * k + 127 : 128 * k + 128], (1, 128)) for k in range(NX)]
    prior = jnp.broadcast_to(ids[1, :, 511:512], (1, 128))
    prior = jnp.where(z == 0, jnp.full_like(prior, -1.0), prior)
    for k in range(1, NX):
        prior = jnp.where(x == k, last[k - 1], prior)
    column = jnp.transpose(jnp.broadcast_to(ids_ref[...], (128, 128)))
    before = pltpu.roll(column, 1, axis=0)
    before = jnp.where(iota((128, 128), 0) == 0, jnp.broadcast_to(prior, (128, 128)), before)
    linked = column == before
    for k in range(4):
        cols = slice(128 * k, 128 * k + 128)
        dt2[:, cols] = jnp.where(linked, step[:, cols], RESET)
    ss[x] = jnp.sum(dt2[...], axis=0, keepdims=True)
    slot_ss = links.slots(4)
    for dx in range(1, NX):
        links.start(ss.at[x], ss.at[x], (z, xat(dx), y, c), slot_ss + dx)

    driven = (step * values).astype(BF16)
    pick = (lax.rem(iota((256, 128), 0), STATE) == iota((256, 128), 1)).astype(BF16)
    inputs = nt(pick, sb[:, RANK:])

    def fill(k, _):
        token = iota((256, 128), 0) // STATE + k * 16
        spread_in = jnp.where(iota((256, 128), 1) == token, inputs, 0.0).astype(BF16)
        bx[pl.ds(pl.multiple_of(k * 256, 256), 256), :] = nn(spread_in, driven)
        return 0

    lax.fori_loop(0, 8, fill, 0)
    rate = a_ref[...]

    def scan(initial, keep_states):
        def advance(k, h):
            steps = dt2[pl.ds(pl.multiple_of(k * 8, 8), 8), :]
            for j in range(8):
                at = pl.ds(pl.multiple_of(k * 128 + j * 16, 16), 16)
                h = jnp.exp2(rate * steps[j : j + 1, :]) * h + bx[at, :]
                if keep_states:
                    hb[at, :] = h.astype(BF16)
            return h

        return lax.fori_loop(0, 16, advance, initial)

    hs[x] = scan(jnp.zeros((STATE, 512), F32), False).astype(BF16)
    slot_hs = links.slots(4)
    for dx in range(1, NX):
        links.start(hs.at[x], hs.at[x], (z, xat(dx), y, c), slot_hs + dx)
    ring_wait(1, slot_wo, wo_at)
    ring_out(2)
    ring_wait(1, slot_wp, wp_at)
    ring_proj(2)

    for dx in range(1, NX):
        links.wait(ss.at[x], slot_ss + dx, (z, xat(dx), y, c))
        links.wait(hs.at[x], slot_hs + dx, (z, xat(dx), y, c))
    running = jnp.zeros((STATE, 512), F32)
    steps_sum = jnp.zeros((1, 512), F32)
    own_prior, own_steps = running, steps_sum
    for k in range(NX):
        own_prior = jnp.where(x == k, running, own_prior)
        own_steps = jnp.where(x == k, steps_sum, own_steps)
        running = jnp.exp2(rate * ss[k]) * running + hs[k].astype(F32)
        steps_sum = steps_sum + ss[k]
    hr[...] = running.astype(BF16)
    sr[...] = steps_sum
    slot_hz, slot_sz = links.slots(5), links.slots(5)
    for dz in range(1, 5):
        links.start(hr, hz.at[dz - 1], (zat(dz), x, y, c), slot_hz + dz)
        links.start(sr, sz.at[dz - 1], (zat(dz), x, y, c), slot_sz + dz)
    spread([z] + [zat(-d) for d in hops(1)])
    ring_wait(2, slot_wo, wo_at)
    ring_out(3)
    spread([zat(-d) for d in hops(2)])
    for dz in range(1, 5):
        links.wait(hz.at[dz - 1], slot_hz + dz, (zat(dz), x, y, c))
        links.wait(sz.at[dz - 1], slot_sz + dz, (zat(dz), x, y, c))
    above = jnp.zeros((STATE, 512), F32)
    for dz in range(4, 0, -1):
        joined = jnp.exp2(rate * sz[dz - 1]) * above + hz[dz - 1].astype(F32)
        above = jnp.where(z >= dz, joined, jnp.zeros_like(joined))
    carry = jnp.exp2(rate * own_steps) * above + own_prior
    ring_wait(2, slot_wp, wp_at)
    ring_proj(3)
    scan(carry, True)
    ring_wait(3, slot_wo, wo_at)
    ring_out(4)
    spread([zat(-d) for d in hops(3)])
    ring_wait(3, slot_wp, wp_at)
    ring_proj(4)

    pick_out = (lax.rem(iota((256, 128), 0), STATE) + STATE == iota((256, 128), 1)).astype(BF16)
    own_token = iota((16, 256), 1) // STATE == iota((16, 256), 0)

    def contract(k, _):
        rows = pl.ds(pl.multiple_of(k * 16, 16), 16)
        coef = nt(sb[rows, RANK:], pick_out)
        coef = jnp.where(own_token, coef, 0.0).astype(BF16)
        ys[rows, :] = nn(coef, hb[pl.ds(pl.multiple_of(k * 256, 256), 256), :])
        return 0

    lax.fori_loop(0, 8, contract, 0)
    gate = g_ref[...].astype(F32)
    mixed = (ys[...] + skip_ref[...] * values) * (gate / (1.0 + jnp.exp(-gate)))
    gt[...] = mixed.astype(BF16)

    ring_wait(4, slot_wo, wo_at)
    spread([zat(-d) for d in hops(4)])
    for dx in range(1, NX):
        links.wait(xw.at[:, x], slot_xw + dx, (z, xat(dx), y, c))

    def project(target, half, extra):
        rows = pl.ds(pl.multiple_of(64 * half, 64), 64)

        def one(k, _):
            weight = xw[pl.ds(2 * k, 2)].reshape(256, 512)
            product = nt(gt[rows, :], weight)
            cols = pl.ds(pl.multiple_of(k * 256, 256), 256)
            if extra is not None:
                product = product + extra[:, cols].astype(F32)
            target[:, cols] = product.astype(target.dtype)
            return 0

        lax.fori_loop(0, 8, one, 0)

    project(ps, other, None)
    slot_pr = links.slots(1)
    links.start(ps, pr, partner, slot_pr)
    ring_wait(4, slot_wp, wp_at)
    slot_pw = links.slots(1)
    links.start(wp.at[:, ringed], wp.at[:, ringed], partner, slot_pw)
    links.wait(pr, slot_pr, partner)
    project(ow, c, pr)
    r2s[...] = ow[...].astype(BF16)
    slot_r2 = links.slots(4)
    for dy in range(1, NY):
        ty = yat(dy)
        links.start(r2s.at[pl.ds(pl.multiple_of(16 * ty, 16), 16)], r2.at[dy], (z, x, ty, c), slot_r2 + dy)
    stream = ow[pl.ds(pl.multiple_of(16 * y, 16), 16), :] + res_ref[pl.ds(my_rows, 16), :].astype(F32)
    for dy in range(1, NY):
        links.wait(r2.at[dy], slot_r2 + dy, partner)
        stream = stream + r2[dy].astype(F32)
    stream = stream.astype(BF16).astype(F32)
    normed = stream * lax.rsqrt(jnp.mean(stream * stream, axis=-1, keepdims=True) + EPS) * gain_ref[...]
    normed = normed.astype(BF16)

    na[x, y] = normed[:, :1024]
    nb[x, y] = normed[:, 1024:]
    slot_n1, slot_n2, slot_n3, slot_n4 = (links.slots(4) for _ in range(4))
    for d in range(1, 4):
        links.start(na.at[x, y], na.at[x, y], (z, xat(d), y, c), slot_n1 + d)
        links.start(nb.at[x, y], nb.at[x, y], (z, x, yat(d), c), slot_n2 + d)
    for d in range(1, 4):
        links.wait(na.at[x, y], slot_n1 + d, partner)
    for d in range(1, 4):
        links.start(na.at[:, y], na.at[:, y], (z, x, yat(d), c), slot_n3 + d)
    for d in range(1, 4):
        links.wait(nb.at[x, y], slot_n2 + d, partner)
    for d in range(1, 4):
        links.start(nb.at[x], nb.at[x], (z, xat(d), y, c), slot_n4 + d)

    for k in range(NX):
        qd[k] = jnp.transpose(jnp.broadcast_to(ids[0, :, 128 * k : 128 * k + 128], (128, 128)))
    half_rows = pl.ds(pl.multiple_of(64 * c, 64), 64)
    q_doc = jnp.concatenate([qd[k, half_rows, :] for k in range(NX)], axis=0)
    q_doc = jnp.concatenate([q_doc] * 4, axis=1)
    row_of = iota((256, 512), 0)
    q_pos = 512 * z + 128 * (row_of // 64) + 64 * c + lax.rem(row_of, 64)

    links.wait(wp.at[:, ringed], slot_pw, partner)
    for d in range(1, 4):
        links.wait(na.at[:, y], slot_n3 + d, partner)
    for d in range(1, 4):
        links.wait(nb.at[x], slot_n4 + d, partner)
    triple = nn(na[...].reshape(256, 1024), wp[0:8].reshape(1024, 384))
    triple = triple + nn(nb[...].reshape(256, 1024), wp[8:16].reshape(1024, 384))
    query = triple[:, :HEAD].astype(BF16)
    kv[0, :, c] = triple[:, HEAD:].astype(BF16).reshape(4, 64, 256)

    slot_kz = [links.slots(2) for _ in range(5)]
    slot_kc = [links.slots(2) for _ in range(5)]

    def chunk(d, part_of, core):
        return kv.at[d, pl.ds(2 * part_of, 2), core]

    def pass_on(d, part_of):
        if d < 4:
            links.start(chunk(d, part_of, c), chunk(d + 1, part_of, c), (zat(1), x, y, c), slot_kz[d + 1] + part_of)
        links.start(chunk(d, part_of, c), chunk(d, part_of, c), partner, slot_kc[d] + part_of)

    top = jnp.full((256, 1), HIDDEN, F32)
    mass = jnp.zeros((256, 1), F32)
    acc = jnp.zeros((256, HEAD), F32)

    def attend(d, carried):
        top, mass, acc = carried
        for p in range(2):
            links.wait(chunk(d, p, other), slot_kc[d] + p, partner)
        block = kv[d].reshape(512, 256)
        scores = nt(query, block[:, :HEAD]) * HEAD**-0.5
        k_pos = 512 * (z - d) + iota((256, 512), 1)
        k_doc = jnp.broadcast_to(ids[d], (256, 512))
        allowed = (k_pos >= 0) & (k_pos <= q_pos) & (k_pos > q_pos - WINDOW) & (k_doc == q_doc)
        scores = jnp.where(allowed, scores, HIDDEN)
        new_top = jnp.maximum(top, jnp.max(scores, axis=-1, keepdims=True))
        probs = jnp.exp(scores - new_top)
        shrink = jnp.exp(top - new_top)
        mass = mass * shrink + jnp.sum(probs, axis=-1, keepdims=True)
        acc = acc * shrink + nn(probs.astype(BF16), block[:, HEAD:])
        return new_top, mass, acc

    carried = (top, mass, acc)
    for p in range(2):
        pass_on(0, p)
    for d in range(1, 5):
        for p in range(2):
            links.wait(chunk(d, p, c), slot_kz[d] + p, partner)
            pass_on(d, p)
        carried = attend(d - 1, carried)
    top, mass, acc = attend(4, carried)
    ob[...] = (acc / mass).astype(BF16).reshape(4, 64, HEAD)

    slot_o = links.slots(4)
    mine = slot_o + lax.rem(x, 2) * 2 + c
    cols = pl.ds(pl.multiple_of(128 * lax.rem(x, 2), 128), 128)
    for dx in range(1, NX):
        tx = xat(dx)
        links.start(ob.at[tx], outb.at[half_rows, cols], (z, tx, y, x // 2), mine)
    stays = c == x // 2
    to_partner = links.copy(ob.at[x], outb.at[half_rows, cols], partner, mine)

    @pl.when(stays)
    def _():
        outb[half_rows, cols] = ob[x]

    @pl.when(jnp.logical_not(stays))
    def _():
        to_partner.start()

    for k in range(4):
        from_me = stays & (lax.rem(x, 2) * 2 + c == k)

        @pl.when(jnp.logical_not(from_me))
        def _():
            links.wait(outb.at[half_rows, cols], slot_o + k, partner)

    out_ref[...] = outb[...]

    @pl.when(jnp.logical_not(stays))
    def _():
        to_partner.wait_send()

    links.drain()
    for dx in range(1, NX):
        links.copy(xw.at[:, x], xw.at[:, x], (z, xat(dx), y, c), slot_xw + dx, first_xw + dx - 1).wait_send()
    assert links.sends <= SENDS and links.recvs <= RECVS, (links.sends, links.recvs)


SENDS, RECVS = 160, 160


def body(
    mixer_input, gate_input, document_ids, residual, select_weight, step_weight, step_bias, decay_log, skip_gain,
    out_weight, norm_gain, project_weight,
):
    vmem = pl.BlockSpec(memory_space=pltpu.VMEM)
    operands = (
        mixer_input,
        gate_input,
        document_ids.astype(F32).reshape(1, 128),
        residual,
        jnp.pad(select_weight, ((0, 0), (0, 96))),
        step_weight,
        step_bias.reshape(1, 512),
        -jnp.exp(decay_log).T * LOG2E,
        skip_gain.reshape(1, 512),
        out_weight.T,
        norm_gain.reshape(1, 2048),
        project_weight.reshape(32, 3, 2, 128).transpose(2, 0, 1, 3).reshape(2, 32, 384),
    )
    scratch = [
        pltpu.VMEM((128, 256), F32),
        pltpu.VMEM((8, 16, 256), F32),
        pltpu.VMEM((128, 256), BF16),
        pltpu.VMEM((5, 1, 512), F32),
        pltpu.VMEM((128, 512), F32),
        pltpu.VMEM((2048, 512), F32),
        pltpu.VMEM((2048, 512), BF16),
        pltpu.VMEM((4, 16, 512), BF16),
        pltpu.VMEM((4, 1, 512), F32),
        pltpu.VMEM((4, 16, 512), BF16),
        pltpu.VMEM((4, 1, 512), F32),
        pltpu.VMEM((16, 512), BF16),
        pltpu.VMEM((1, 512), F32),
        pltpu.VMEM((16, 4, 32, 512), BF16),
        pltpu.VMEM((16, 4, 32, 384), BF16),
        pltpu.VMEM((128, 512), F32),
        pltpu.VMEM((128, 512), BF16),
        pltpu.VMEM((64, 2048), BF16),
        pltpu.VMEM((64, 2048), BF16),
        pltpu.VMEM((64, 2048), F32),
        pltpu.VMEM((64, 2048), BF16),
        pltpu.VMEM((4, 16, 2048), BF16),
        pltpu.VMEM((4, 4, 16, 1024), BF16),
        pltpu.VMEM((4, 4, 16, 1024), BF16),
        pltpu.VMEM((5, 4, 2, 64, 256), BF16),
        pltpu.VMEM((4, 128, 128), F32),
        pltpu.VMEM((4, 64, 128), BF16),
        pltpu.VMEM((128, 256), BF16),
        pltpu.SemaphoreType.DMA((SENDS,)),
        pltpu.SemaphoreType.DMA((RECVS,)),
    ]
    return pl.pallas_call(
        kernel,
        out_shape=jax.ShapeDtypeStruct((128, 256), BF16),
        in_specs=[vmem] * len(operands),
        out_specs=vmem,
        scratch_shapes=scratch,
        compiler_params=pltpu.CompilerParams(collective_id=0, has_side_effects=True, vmem_limit_bytes=48 << 20),
    )(*operands)


def solution(mesh):
    split = Mesh(mesh.devices.reshape(NZ, NX, NY, NC), ("z", "x", "y", "c"))
    placed = (
        P(SEQ, TP), P(SEQ, TP), P(SEQ), P(SEQ, None), P(TP, None), P(None, TP), P(TP), P(TP, None), P(TP),
        P(TP, SEQ), P(), P(SEQ, None, TP),
    )
    return jax.shard_map(body, mesh=split, in_specs=placed, out_specs=P(SEQ, TP), check_vma=False)
```

time: 618 us -> 105 us (0.17)
  the two profiles are of different devices: /device:TPU:128 before, /device:TPU:1 now
where the time goes in v1:
time: 105 us
  Pallas kernels  101 us (96%)
  local copies, waits for them, and re-layouts  3.28 us (3%)
    pallas_call x1, Pallas kernels, body(): pl.pallas_call(kernel, out_shape=jax.ShapeDtypeStruct((128, 256), BF16),...  101 us
    unnamed x24, local copies, waits for them, and re-layouts  3.13 us

profile of v1, /device:TPU:1, one launch (start us, length us, event | category | flops | bytes accessed | tf_op | source)
XLA Modules:
  0.0 104.6 jit_solution(8427809097968865194)
XLA Ops:
  0.0 0.0 copy-start.8
  0.0 0.0 copy-start.9
  0.0 0.0 copy-start.7
  0.0 1.1 %copy.15 = bf16[512,160]{1,0:T(8,128)(2,1)S(1)} copy(bf16[512,160]{0,1:T(8,128)(2,1)} %param.16) | data formatting | bytes 327680 | tf_op args[4]
  1.1 0.0 copy-start
  1.2 0.0 copy-done.8
  1.2 0.0 copy-start.3
  1.2 0.0 copy-start.1
  1.2 0.0 copy-start.2
  1.3 0.0 copy-start.10
  1.3 0.1 reshape.23.wp_ref
  1.3 0.0 copy-done.9
  1.4 0.0 copy-start.6
  1.4 0.6 copy-done.10
  2.0 0.0 copy-done.4
  2.0 0.0 copy-done.7
  2.0 0.1 copy-done
  2.1 0.0 copy-done.3
  2.2 0.0 copy-done.1
  2.2 0.1 copy-done.2
  2.3 0.0 copy-done.6
  2.3 0.5 copy-done.5
  2.8 101.2 %shard_map.118 = bf16[128,256]{1,0:T(8,128)(2,1)S(1)} custom-call(bf16[128,512]{1,0:T(8,128)(2,1)S(1)} %copy-done.1, bf16[128,512]{1,0:T(8,128)(2,1)S(1)} %copy-done.2, f32[1,128]{1,0:T(1,128)S(1)} %convert_bitcast_fusion.ids_ref, bf16[128,2048]{1,0:T(8,128)(2,1)S(1)} %copy-done, bf16[512,256]{1,0:T(8,128)(2,1)S(1)} %pad.4.sel_ref, ...), custom_call_target="tpu_custom_call" | custom-call | tf_op jit(solution)/shard_map/pallas_call | solution.py:531
  103.9 0.6 copy.20
  (7 shorter events, 0.1 us)
Async XLA Ops:
  0.0 1.2 %copy-start.8 = (bf16[32,3,256]{2,0,1:T(8,128)(2,1)S(1)}, bf16[32,3,256]{2,0,1:T(8,128)(2,1)}, u32[]{:S(2)}) copy-start(bf16[32,3,256]{2,0,1:T(8,128)(2,1)} %param.23) | copy-start | bytes 147460
  0.0 1.3 %copy-start.9 = (f32[512,16]{0,1:T(8,128)S(1)}, f32[512,16]{0,1:T(8,128)}, u32[]{:S(2)}) copy-start(f32[512,16]{0,1:T(8,128)} %param.19) | copy-start | bytes 98308
  0.0 2.0 %copy-start.4 = (bf16[512,32]{0,1:T(8,128)(2,1)S(1)}, bf16[512,32]{0,1:T(8,128)(2,1)}, u32[]{:S(2)}) copy-start(bf16[512,32]{0,1:T(8,128)(2,1)} %param.21) | copy-start | bytes 98308
  0.0 2.0 %copy-start.7 = (f32[512]{0:T(512)S(1)}, f32[512]{0:T(512)}, u32[]{:S(2)}) copy-start(f32[512]{0:T(512)} %param.20) | copy-start | bytes 6148
  1.1 1.0 copy-start
  1.2 1.0 copy-start.3
  1.2 1.0 copy-start.1
  1.2 1.1 %copy-start.2 = (bf16[128,512]{1,0:T(8,128)(2,1)S(1)}, bf16[128,512]{1,0:T(8,128)(2,1)}, u32[]{:S(2)}) copy-start(bf16[128,512]{1,0:T(8,128)(2,1)} %g_ref.1) | copy-start | bytes 393220
  1.3 0.7 copy-start.10
  1.4 0.9 copy-start.6
  2.0 0.8 copy-start.5

commit v2 on v1

--- a/solution.py
+++ b/solution.py
@@ -80,7 +80,7 @@
 def kernel(
     x_ref, g_ref, ids_ref, res_ref, sel_ref, stepw_ref, bias_ref, a_ref, skip_ref, wo_ref, gain_ref, wp_ref,
     out_ref,
-    part, rs1, sb, ids, dt2, bx, hb, hs, ss, hz, sz, hr, sr, xw, wp, ys, gt, ps, pr, ow, r2s, r2, na, nb,
+    part, part16, rs1, sb, ids, dt2, bx, hb, hs, ss, hz, sz, hr, sr, xw, wp, ys, gt, ps, pr, ow, r2s, r2, na, nb,
     kv, qd, ob, outb, send_sem, recv_sem,
 ):
     z, x, y, c = (lax.axis_index(n) for n in ("z", "x", "y", "c"))
@@ -107,11 +107,12 @@
         pl.semaphore_signal(barrier, inc=1, device_id=device, device_id_type=MESH)
 
     links = Links(send_sem, recv_sem)
-    me = (z, x, y, c)
     partner = (z, x, y, other)
     my_rows = pl.multiple_of(64 * c + 16 * y, 16)
 
-    part[...] = nn(x_ref[...], sel_ref[...])
+    partial = nn(x_ref[...], sel_ref[...])
+    part[...] = partial
+    part16[...] = partial.astype(BF16)
     xw[z, x] = wo_ref[...]
     ids[0, :, pl.ds(pl.multiple_of(128 * x, 128), 128)] = ids_ref[...]
     pl.semaphore_wait(barrier, len(everyone))
@@ -122,7 +123,7 @@
             if dy or dc:
                 ty, tc = yat(dy), cat(dc)
                 rows = pl.multiple_of(64 * tc + 16 * ty, 16)
-                links.start(part.at[pl.ds(rows, 16)], rs1.at[dy * 2 + dc], (z, x, ty, tc), slot_rs + dy * 2 + dc)
+                links.start(part16.at[pl.ds(rows, 16)], rs1.at[dy * 2 + dc], (z, x, ty, tc), slot_rs + dy * 2 + dc)
 
     slot_x0 = links.slots(2)
     for hh in range(2):
@@ -177,23 +178,30 @@
     def wp_at(block):
         return wp.at[block, ringed]
 
-    slot_xw = links.slots(4)
-    first_xw = links.sends
-    links.sends += 3
-
-    def spread(blocks):
-        for block in blocks:
+    groups = [[0, -1, 1, -2, 2], [-3, 3, -4, 4], [-5, 5, -6, 6], [-7, 7, 8]]
+    slot_xw = [links.slots(4) for _ in groups]
+    first_xw = [links.sends + 3 * g for g in range(len(groups))]
+    links.sends += 3 * len(groups)
+
+    def spread(g, members):
+        for d in members:
+            block = zat(-d)
             for dx in range(1, NX):
                 links.copy(
-                    xw.at[block, x], xw.at[block, x], (z, xat(dx), y, c), slot_xw + dx, first_xw + dx - 1
+                    xw.at[block, x], xw.at[block, x], (z, xat(dx), y, c), slot_xw[g] + dx, first_xw[g] + dx - 1
                 ).start()
 
     ring_out(1)
+    for dx in range(1, NX):
+        links.wait(ids.at[0, :, row_part], slot_i1 + dx, (z, xat(dx), y, c))
+    slot_i2 = links.slots(5)
+    for dz in range(1, 5):
+        links.start(ids.at[0], ids.at[dz], (zat(dz), x, y, c), slot_i2 + dz)
 
     total = part[pl.ds(my_rows, 16), :]
     for k in range(1, 8):
         links.wait(rs1.at[k], slot_rs + k, partner)
-        total = total + rs1[k]
+        total = total + rs1[k].astype(F32)
     sb[pl.ds(my_rows, 16), :] = total.astype(BF16)
     slot_ag = links.slots(8)
     for dy in range(NY):
@@ -202,13 +210,11 @@
                 mine = sb.at[pl.ds(my_rows, 16)]
                 links.start(mine, mine, (z, x, yat(dy), cat(dc)), slot_ag + dy * 2 + dc)
 
-    for dx in range(1, NX):
-        links.wait(ids.at[0, :, row_part], slot_i1 + dx, (z, xat(dx), y, c))
-    slot_i2 = links.slots(5)
-    for dz in range(1, 5):
-        links.start(ids.at[0], ids.at[dz], (zat(dz), x, y, c), slot_i2 + dz)
     for k in range(2):
         links.wait(wp.at[z, x], slot_x0 + k, partner)
+    ring_wait(1, slot_wo, wo_at)
+    ring_out(2)
+    spread(0, groups[0][:4])
     ring_proj(1)
 
     for k in range(1, 8):
@@ -239,13 +245,12 @@
     pick = (lax.rem(iota((256, 128), 0), STATE) == iota((256, 128), 1)).astype(BF16)
     inputs = nt(pick, sb[:, RANK:])
 
-    def fill(k, _):
+    for k in range(8):
         token = iota((256, 128), 0) // STATE + k * 16
         spread_in = jnp.where(iota((256, 128), 1) == token, inputs, 0.0).astype(BF16)
-        bx[pl.ds(pl.multiple_of(k * 256, 256), 256), :] = nn(spread_in, driven)
-        return 0
-
-    lax.fori_loop(0, 8, fill, 0)
+        bx[256 * k : 256 * k + 256, :] = nn(spread_in, driven)
+    ring_wait(2, slot_wo, wo_at)
+    ring_out(3)
     rate = a_ref[...]
 
     def scan(initial, keep_states):
@@ -264,11 +269,8 @@
     slot_hs = links.slots(4)
     for dx in range(1, NX):
         links.start(hs.at[x], hs.at[x], (z, xat(dx), y, c), slot_hs + dx)
-    ring_wait(1, slot_wo, wo_at)
-    ring_out(2)
-    ring_wait(1, slot_wp, wp_at)
-    ring_proj(2)
-
+    spread(0, groups[0][4:])
+    spread(1, groups[1])
     for dx in range(1, NX):
         links.wait(ss.at[x], slot_ss + dx, (z, xat(dx), y, c))
         links.wait(hs.at[x], slot_hs + dx, (z, xat(dx), y, c))
@@ -286,10 +288,9 @@
     for dz in range(1, 5):
         links.start(hr, hz.at[dz - 1], (zat(dz), x, y, c), slot_hz + dz)
         links.start(sr, sz.at[dz - 1], (zat(dz), x, y, c), slot_sz + dz)
-    spread([z] + [zat(-d) for d in hops(1)])
-    ring_wait(2, slot_wo, wo_at)
-    ring_out(3)
-    spread([zat(-d) for d in hops(2)])
+    ring_wait(3, slot_wo, wo_at)
+    ring_out(4)
+    spread(2, groups[2])
     for dz in range(1, 5):
         links.wait(hz.at[dz - 1], slot_hz + dz, (zat(dz), x, y, c))
         links.wait(sz.at[dz - 1], slot_sz + dz, (zat(dz), x, y, c))
@@ -298,65 +299,80 @@
         joined = jnp.exp2(rate * sz[dz - 1]) * above + hz[dz - 1].astype(F32)
         above = jnp.where(z >= dz, joined, jnp.zeros_like(joined))
     carry = jnp.exp2(rate * own_steps) * above + own_prior
-    ring_wait(2, slot_wp, wp_at)
-    ring_proj(3)
+    ring_wait(1, slot_wp, wp_at)
+    ring_proj(2)
     scan(carry, True)
-    ring_wait(3, slot_wo, wo_at)
-    ring_out(4)
-    spread([zat(-d) for d in hops(3)])
-    ring_wait(3, slot_wp, wp_at)
-    ring_proj(4)
-
+    ring_wait(4, slot_wo, wo_at)
+    spread(3, groups[3])
     pick_out = (lax.rem(iota((256, 128), 0), STATE) + STATE == iota((256, 128), 1)).astype(BF16)
     own_token = iota((16, 256), 1) // STATE == iota((16, 256), 0)
 
-    def contract(k, _):
-        rows = pl.ds(pl.multiple_of(k * 16, 16), 16)
+    for k in range(8):
+        rows = slice(16 * k, 16 * k + 16)
         coef = nt(sb[rows, RANK:], pick_out)
         coef = jnp.where(own_token, coef, 0.0).astype(BF16)
-        ys[rows, :] = nn(coef, hb[pl.ds(pl.multiple_of(k * 256, 256), 256), :])
-        return 0
-
-    lax.fori_loop(0, 8, contract, 0)
+        ys[rows, :] = nn(coef, hb[256 * k : 256 * k + 256, :])
     gate = g_ref[...].astype(F32)
     mixed = (ys[...] + skip_ref[...] * values) * (gate / (1.0 + jnp.exp(-gate)))
     gt[...] = mixed.astype(BF16)
 
-    ring_wait(4, slot_wo, wo_at)
-    spread([zat(-d) for d in hops(4)])
-    for dx in range(1, NX):
-        links.wait(xw.at[:, x], slot_xw + dx, (z, xat(dx), y, c))
-
-    def project(target, half, extra):
-        rows = pl.ds(pl.multiple_of(64 * half, 64), 64)
-
-        def one(k, _):
-            weight = xw[pl.ds(2 * k, 2)].reshape(256, 512)
-            product = nt(gt[rows, :], weight)
-            cols = pl.ds(pl.multiple_of(k * 256, 256), 256)
-            if extra is not None:
-                product = product + extra[:, cols].astype(F32)
-            target[:, cols] = product.astype(target.dtype)
-            return 0
-
-        lax.fori_loop(0, 8, one, 0)
-
-    project(ps, other, None)
-    slot_pr = links.slots(1)
-    links.start(ps, pr, partner, slot_pr)
-    ring_wait(4, slot_wp, wp_at)
-    slot_pw = links.slots(1)
-    links.start(wp.at[:, ringed], wp.at[:, ringed], partner, slot_pw)
-    links.wait(pr, slot_pr, partner)
-    project(ow, c, pr)
-    r2s[...] = ow[...].astype(BF16)
-    slot_r2 = links.slots(4)
+    slot_pr = [links.slots(1) for _ in groups]
+    slot_r2 = [links.slots(4) for _ in groups]
+    first_pr = [links.sends + g for g in range(len(groups))]
+    first_r2 = [links.sends + len(groups) + 3 * g for g in range(len(groups))]
+    links.sends += 4 * len(groups)
+    half_rows = pl.ds(pl.multiple_of(64 * c, 64), 64)
+    their_rows = pl.ds(pl.multiple_of(64 * other, 64), 64)
+
+    def columns(d):
+        return pl.ds(pl.multiple_of(128 * zat(-d), 128), 128)
+
+    def weight_of(d):
+        return xw[zat(-d)].reshape(128, 512)
+
+    def project_pair(g):
+        for d in groups[g]:
+            ps[:, columns(d)] = nt(gt[their_rows, :], weight_of(d)).astype(BF16)
+        for d in groups[g]:
+            piece = ps.at[:, columns(d)]
+            links.copy(piece, pr.at[:, columns(d)], partner, slot_pr[g], first_pr[g]).start()
+
+    def project_own(g):
+        for d in groups[g]:
+            ow[:, columns(d)] = nt(gt[half_rows, :], weight_of(d))
+        width = 128 * len(groups[g])
+        links.copy(ps.at[:, 0:width], pr.at[:, 0:width], partner, slot_pr[g], first_pr[g]).wait_recv()
+        for d in groups[g]:
+            joined = ow[:, columns(d)] + pr[:, columns(d)].astype(F32)
+            ow[:, columns(d)] = joined
+            r2s[:, columns(d)] = joined.astype(BF16)
+        for d in groups[g]:
+            for dy in range(1, NY):
+                ty = yat(dy)
+                piece = r2s.at[pl.ds(pl.multiple_of(16 * ty, 16), 16), columns(d)]
+                links.copy(
+                    piece, r2.at[dy, :, columns(d)], (z, x, ty, c), slot_r2[g] + dy, first_r2[g] + dy - 1
+                ).start()
+
+    for g in range(len(groups)):
+        size = len(groups[g])
+        for dx in range(1, NX):
+            links.copy(
+                xw.at[0:size, x], xw.at[0:size, x], (z, xat(dx), y, c), slot_xw[g] + dx, first_xw[g] + dx - 1
+            ).wait_recv()
+        project_pair(g)
+        if g == 1:
+            ring_wait(2, slot_wp, wp_at)
+            ring_proj(3)
+        project_own(g)
+    ring_wait(3, slot_wp, wp_at)
+    ring_proj(4)
+    stream = ow[pl.ds(pl.multiple_of(16 * y, 16), 16), :] + res_ref[pl.ds(my_rows, 16), :].astype(F32)
+    for g in range(len(groups)):
+        width = 128 * len(groups[g])
+        for dy in range(1, NY):
+            links.wait(r2.at[dy, :, 0:width], slot_r2[g] + dy, partner)
     for dy in range(1, NY):
-        ty = yat(dy)
-        links.start(r2s.at[pl.ds(pl.multiple_of(16 * ty, 16), 16)], r2.at[dy], (z, x, ty, c), slot_r2 + dy)
-    stream = ow[pl.ds(pl.multiple_of(16 * y, 16), 16), :] + res_ref[pl.ds(my_rows, 16), :].astype(F32)
-    for dy in range(1, NY):
-        links.wait(r2.at[dy], slot_r2 + dy, partner)
         stream = stream + r2[dy].astype(F32)
     stream = stream.astype(BF16).astype(F32)
     normed = stream * lax.rsqrt(jnp.mean(stream * stream, axis=-1, keepdims=True) + EPS) * gain_ref[...]
@@ -364,42 +380,55 @@
 
     na[x, y] = normed[:, :1024]
     nb[x, y] = normed[:, 1024:]
-    slot_n1, slot_n2, slot_n3, slot_n4 = (links.slots(4) for _ in range(4))
+    slot_n1, slot_n2 = links.slots(4), links.slots(4)
+    slot_n3 = [links.slots(4) for _ in range(4)]
+    slot_n4 = [links.slots(4) for _ in range(4)]
     for d in range(1, 4):
         links.start(na.at[x, y], na.at[x, y], (z, xat(d), y, c), slot_n1 + d)
         links.start(nb.at[x, y], nb.at[x, y], (z, x, yat(d), c), slot_n2 + d)
-    for d in range(1, 4):
-        links.wait(na.at[x, y], slot_n1 + d, partner)
-    for d in range(1, 4):
-        links.start(na.at[:, y], na.at[:, y], (z, x, yat(d), c), slot_n3 + d)
-    for d in range(1, 4):
-        links.wait(nb.at[x, y], slot_n2 + d, partner)
-    for d in range(1, 4):
-        links.start(nb.at[x], nb.at[x], (z, xat(d), y, c), slot_n4 + d)
-
+
+    def over_y(k):
+        piece = na.at[xat(k), y]
+        for d in range(1, 4):
+            links.start(piece, piece, (z, x, yat(d), c), slot_n3[k] + d)
+
+    def over_x(k):
+        piece = nb.at[x, yat(k)]
+        for d in range(1, 4):
+            links.start(piece, piece, (z, xat(d), y, c), slot_n4[k] + d)
+
+    over_y(0)
+    over_x(0)
+    for k in (3, 1, 2):
+        links.wait(na.at[x, y], slot_n1 + 4 - k, partner)
+        over_y(k)
+        links.wait(nb.at[x, y], slot_n2 + 4 - k, partner)
+        over_x(k)
+    ring_wait(4, slot_wp, wp_at)
+    slot_pw = links.slots(1)
+    links.start(wp.at[:, ringed], wp.at[:, ringed], partner, slot_pw)
     for k in range(NX):
         qd[k] = jnp.transpose(jnp.broadcast_to(ids[0, :, 128 * k : 128 * k + 128], (128, 128)))
-    half_rows = pl.ds(pl.multiple_of(64 * c, 64), 64)
     q_doc = jnp.concatenate([qd[k, half_rows, :] for k in range(NX)], axis=0)
     q_doc = jnp.concatenate([q_doc] * 4, axis=1)
     row_of = iota((256, 512), 0)
-    q_pos = 512 * z + 128 * (row_of // 64) + 64 * c + lax.rem(row_of, 64)
+    in_row = 128 * (row_of // 64) + 64 * c + lax.rem(row_of, 64)
 
     links.wait(wp.at[:, ringed], slot_pw, partner)
-    for d in range(1, 4):
-        links.wait(na.at[:, y], slot_n3 + d, partner)
-    for d in range(1, 4):
-        links.wait(nb.at[x], slot_n4 + d, partner)
+    for k in range(4):
+        for d in range(1, 4):
+            links.wait(na.at[x, y], slot_n3[k] + d, partner)
+            links.wait(nb.at[x, y], slot_n4[k] + d, partner)
     triple = nn(na[...].reshape(256, 1024), wp[0:8].reshape(1024, 384))
     triple = triple + nn(nb[...].reshape(256, 1024), wp[8:16].reshape(1024, 384))
     query = triple[:, :HEAD].astype(BF16)
     kv[0, :, c] = triple[:, HEAD:].astype(BF16).reshape(4, 64, 256)
 
-    slot_kz = [links.slots(2) for _ in range(5)]
-    slot_kc = [links.slots(2) for _ in range(5)]
+    slot_kz = [links.slots(4) for _ in range(5)]
+    slot_kc = [links.slots(4) for _ in range(5)]
 
     def chunk(d, part_of, core):
-        return kv.at[d, pl.ds(2 * part_of, 2), core]
+        return kv.at[d, part_of, core]
 
     def pass_on(d, part_of):
         if d < 4:
@@ -412,26 +441,30 @@
 
     def attend(d, carried):
         top, mass, acc = carried
-        for p in range(2):
+        for p in range(4):
             links.wait(chunk(d, p, other), slot_kc[d] + p, partner)
         block = kv[d].reshape(512, 256)
-        scores = nt(query, block[:, :HEAD]) * HEAD**-0.5
-        k_pos = 512 * (z - d) + iota((256, 512), 1)
-        k_doc = jnp.broadcast_to(ids[d], (256, 512))
-        allowed = (k_pos >= 0) & (k_pos <= q_pos) & (k_pos > q_pos - WINDOW) & (k_doc == q_doc)
+        scores = nt(query, block[:, :HEAD]) * (HEAD**-0.5 * LOG2E)
+        k_doc = jnp.where(z >= d, ids[d], -1.0)
+        allowed = jnp.broadcast_to(k_doc, (256, 512)) == q_doc
+        ahead = iota((256, 512), 1) - in_row
+        if d == 0:
+            allowed = allowed & (ahead <= 0)
+        if d == 4:
+            allowed = allowed & (ahead > 0)
         scores = jnp.where(allowed, scores, HIDDEN)
         new_top = jnp.maximum(top, jnp.max(scores, axis=-1, keepdims=True))
-        probs = jnp.exp(scores - new_top)
-        shrink = jnp.exp(top - new_top)
+        probs = jnp.exp2(scores - new_top)
+        shrink = jnp.exp2(top - new_top)
         mass = mass * shrink + jnp.sum(probs, axis=-1, keepdims=True)
         acc = acc * shrink + nn(probs.astype(BF16), block[:, HEAD:])
         return new_top, mass, acc
 
     carried = (top, mass, acc)
-    for p in range(2):
+    for p in range(4):
         pass_on(0, p)
     for d in range(1, 5):
-        for p in range(2):
+        for p in range(4):
             links.wait(chunk(d, p, c), slot_kz[d] + p, partner)
             pass_on(d, p)
         carried = attend(d - 1, carried)
@@ -469,12 +502,17 @@
         to_partner.wait_send()
 
     links.drain()
-    for dx in range(1, NX):
-        links.copy(xw.at[:, x], xw.at[:, x], (z, xat(dx), y, c), slot_xw + dx, first_xw + dx - 1).wait_send()
+    for g in range(len(groups)):
+        size, width = len(groups[g]), 128 * len(groups[g])
+        for d in range(1, 4):
+            links.copy(xw.at[0:size, x], xw.at[0:size, x], partner, slot_xw[g] + d, first_xw[g] + d - 1).wait_send()
+            rows = r2.at[d, :, 0:width]
+            links.copy(rows, rows, partner, slot_r2[g] + d, first_r2[g] + d - 1).wait_send()
+        links.copy(ps.at[:, 0:width], pr.at[:, 0:width], partner, slot_pr[g], first_pr[g]).wait_send()
     assert links.sends <= SENDS and links.recvs <= RECVS, (links.sends, links.recvs)
 
 
-SENDS, RECVS = 160, 160
+SENDS, RECVS = 224, 240
 
 
 def body(
@@ -498,7 +536,8 @@
     )
     scratch = [
         pltpu.VMEM((128, 256), F32),
-        pltpu.VMEM((8, 16, 256), F32),
+        pltpu.VMEM((128, 256), BF16),
+        pltpu.VMEM((8, 16, 256), BF16),
         pltpu.VMEM((128, 256), BF16),
         pltpu.VMEM((5, 1, 512), F32),
         pltpu.VMEM((128, 512), F32),

time: 105 us -> 88 us (0.84)
  Pallas kernels: 101 us -> 84.4 us
    pallas_call x1, Pallas kernels: 101 us -> 84.4 us  [body(): pl.pallas_call(kernel, out_shape=jax.ShapeDtypeStruct((128, 256), BF16),...]
where the time goes in v2:
time: 88 us; the launch traced here: 87.9 us
  Pallas kernels  84.4 us (96%)
  local copies, waits for them, and re-layouts  3.28 us (4%)
    pallas_call x1, Pallas kernels, body(): pl.pallas_call(kernel, out_shape=jax.ShapeDtypeStruct((128, 256), BF16),...  84.4 us
    unnamed x24, local copies, waits for them, and re-layouts  3.13 us

profile of v2, /device:TPU:1, one launch (start us, length us, event | category | flops | bytes accessed | tf_op | source)
XLA Modules:
  0.0 87.9 jit_solution(18007629780878053364)
XLA Ops:
  0.0 0.0 copy-start.8
  0.0 0.0 copy-start.9
  0.0 0.0 copy-start.7
  0.0 1.1 %copy.15 = bf16[512,160]{1,0:T(8,128)(2,1)S(1)} copy(bf16[512,160]{0,1:T(8,128)(2,1)} %param.16) | data formatting | bytes 327680 | tf_op args[4]
  1.1 0.0 copy-start
  1.2 0.0 copy-done.8
  1.2 0.0 copy-start.3
  1.2 0.0 copy-start.1
  1.2 0.0 copy-start.2
  1.3 0.0 copy-start.10
  1.3 0.1 reshape.23.wp_ref
  1.3 0.0 copy-done.9
  1.4 0.0 copy-start.6
  1.4 0.6 copy-done.10
  2.0 0.0 copy-done.4
  2.0 0.0 copy-done.7
  2.0 0.1 copy-done
  2.1 0.0 copy-done.3
  2.2 0.0 copy-done.1
  2.2 0.1 copy-done.2
  2.3 0.0 copy-done.6
  2.3 0.5 copy-done.5
  2.8 84.4 %shard_map.118 = bf16[128,256]{1,0:T(8,128)(2,1)S(1)} custom-call(bf16[128,512]{1,0:T(8,128)(2,1)S(1)} %copy-done.1, bf16[128,512]{1,0:T(8,128)(2,1)S(1)} %copy-done.2, f32[1,128]{1,0:T(1,128)S(1)} %convert_bitcast_fusion.ids_ref, bf16[128,2048]{1,0:T(8,128)(2,1)S(1)} %copy-done, bf16[512,256]{1,0:T(8,128)(2,1)S(1)} %pad.4.sel_ref, ...), custom_call_target="tpu_custom_call" | custom-call | tf_op jit(solution)/shard_map/pallas_call | solution.py:570
  87.2 0.6 copy.20
  (7 shorter events, 0.1 us)
Async XLA Ops:
  0.0 1.2 %copy-start.8 = (bf16[32,3,256]{2,0,1:T(8,128)(2,1)S(1)}, bf16[32,3,256]{2,0,1:T(8,128)(2,1)}, u32[]{:S(2)}) copy-start(bf16[32,3,256]{2,0,1:T(8,128)(2,1)} %param.23) | copy-start | bytes 147460
  0.0 1.3 %copy-start.9 = (f32[512,16]{0,1:T(8,128)S(1)}, f32[512,16]{0,1:T(8,128)}, u32[]{:S(2)}) copy-start(f32[512,16]{0,1:T(8,128)} %param.19) | copy-start | bytes 98308
  0.0 2.0 %copy-start.4 = (bf16[512,32]{0,1:T(8,128)(2,1)S(1)}, bf16[512,32]{0,1:T(8,128)(2,1)}, u32[]{:S(2)}) copy-start(bf16[512,32]{0,1:T(8,128)(2,1)} %param.21) | copy-start | bytes 98308
  0.0 2.0 %copy-start.7 = (f32[512]{0:T(512)S(1)}, f32[512]{0:T(512)}, u32[]{:S(2)}) copy-start(f32[512]{0:T(512)} %param.20) | copy-start | bytes 6148
  1.1 1.0 %copy-start = (bf16[128,2048]{1,0:T(8,128)(2,1)S(1)}, bf16[128,2048]{1,0:T(8,128)(2,1)}, u32[]{:S(2)}) copy-start(bf16[128,2048]{1,0:T(8,128)(2,1)} %res_ref.1) | copy-start | bytes 1572868
  1.2 1.0 %copy-start.3 = (bf16[128,512]{1,0:T(8,128)(2,1)S(1)}, bf16[128,512]{1,0:T(8,128)(2,1)}, u32[]{:S(2)}) copy-start(bf16[128,512]{1,0:T(8,128)(2,1)} %stepw_ref.1) | copy-start | bytes 393220
  1.2 1.0 %copy-start.1 = (bf16[128,512]{1,0:T(8,128)(2,1)S(1)}, bf16[128,512]{1,0:T(8,128)(2,1)}, u32[]{:S(2)}) copy-start(bf16[128,512]{1,0:T(8,128)(2,1)} %x_ref.1) | copy-start | bytes 393220
  1.2 1.1 %copy-start.2 = (bf16[128,512]{1,0:T(8,128)(2,1)S(1)}, bf16[128,512]{1,0:T(8,128)(2,1)}, u32[]{:S(2)}) copy-start(bf16[128,512]{1,0:T(8,128)(2,1)} %g_ref.1) | copy-start | bytes 393220
  1.3 0.7 copy-start.10
  1.4 0.9 %copy-start.6 = (f32[512]{0:T(512)S(1)}, f32[512]{0:T(512)}, u32[]{:S(2)}) copy-start(f32[512]{0:T(512)} %param.18) | copy-start | bytes 6148
  2.0 0.8 copy-start.5

commit v3 on v2

v3 whole, which is shorter than its diff:
```python
import math

import jax
import jax.numpy as jnp
from jax import lax
from jax.experimental import pallas as pl
from jax.experimental.pallas import tpu as pltpu
from jax.sharding import Mesh
from jax.sharding import PartitionSpec as P

MESH = pl.DeviceIdType.MESH
NZ, NX, NY, NC = 16, 4, 4, 2
STATE = 16
RANK = 128
HEAD = 128
WINDOW = 2048
EPS = 1e-05
LOG2E = 1.4426950408889634
RESET = 1e6
HIDDEN = -1e30
SEQ = ("z", "x")
TP = ("y", "c")
F32 = jnp.float32
BF16 = jnp.bfloat16


def nt(a, b):
    return lax.dot_general(a, b, (((1,), (1,)), ((), ())), preferred_element_type=F32)


def nn(a, b):
    return jnp.dot(a, b, preferred_element_type=F32)


def iota(shape, dim):
    return lax.broadcasted_iota(jnp.int32, shape, dim)


def softplus(v):
    e = jnp.exp(-jnp.abs(v))
    small = e * (1.0 - e * (0.5 - e * (1.0 / 3.0 - e * 0.25)))
    return jnp.maximum(v, 0.0) + jnp.where(e < 0.01, small, jnp.log(1.0 + e))


class Links:
    def __init__(self, send, recv):
        self.send, self.recv = send, recv
        self.recvs = 0
        self.sent = [0] * SENDS

    def slots(self, count):
        first = self.recvs
        self.recvs += count
        return first

    def copy(self, src, dst, device, slot, send):
        return pltpu.make_async_remote_copy(
            src_ref=src,
            dst_ref=dst,
            send_sem=self.send.at[send],
            recv_sem=self.recv.at[slot],
            device_id=device,
            device_id_type=MESH,
        )

    def start(self, src, dst, device, slot, send=None):
        size = math.prod(src.shape) * jnp.dtype(src.dtype).itemsize
        if send is None:
            send = 0 if self.sent[0] + size <= SEND_MOST else 1
        self.sent[send] += size
        self.copy(src, dst, device, slot, send).start()

    def wait(self, dst, slot, device):
        self.copy(dst, dst, device, slot, 0).wait_recv()

    def drain(self, send, whole, device):
        self.copy(whole, whole, device, 0, send).wait_send()


def kernel(
    *refs
):
    homes, refs = refs[:12], refs[12:]
    out_ref, refs = refs[0], refs[1:]
    staged, refs = refs[:12], refs[12:]
    x_ref, g_ref, doc_ref, res_ref, sel_ref, stepw_ref, bias_ref, a_ref, skip_ref, wo_ref, gain_ref, proj_ref = staged
    (
        part, part2, parts, ids_ref, wp_ref, ids, dt2, bx, hb, hs, ss, hz, sz, hr, sr, xw, wp, ys, gt, ps, pr, ow, r2s, r2, na, nb,
        kv, qd, ob, outb, local_sem, send_sem, recv_sem,
    ) = refs
    z, x, y, c = (lax.axis_index(n) for n in ("z", "x", "y", "c"))
    other = 1 - c

    def zat(d):
        return lax.rem(z + d + NZ, NZ)

    def xat(d):
        return lax.rem(x + d + NX, NX)

    def yat(d):
        return lax.rem(y + d, NY)

    def cat(d):
        return other if d else c

    peers = [(z, x, yat(dy), cat(dc)) for dy in range(NY) for dc in range(NC) if dy or dc]
    row_peers = [(z, xat(dx), y, cat(dc)) for dx in range(1, NX) for dc in range(NC)]
    far = [(zat(d), x, y, c) for d in (-4, -3, -2, -1, 1, 2, 3, 4)]
    barrier = pltpu.get_barrier_semaphore()
    everyone = peers + row_peers + far
    for device in everyone:
        pl.semaphore_signal(barrier, inc=1, device_id=device, device_id_type=MESH)

    links = Links(send_sem, recv_sem)
    loads = [pltpu.make_async_copy(src, dst, local_sem.at[n]) for n, (src, dst) in enumerate(zip(homes, staged))]
    early = (0, 4, 2, 9, 11)
    late = (5, 6, 7, 8, 1, 3, 10)
    for n in early + late:
        loads[n].start()
    partner = (z, x, y, other)
    my_rows = pl.multiple_of(64 * c + 16 * y, 16)

    for n in early:
        loads[n].wait()
    ids_ref[...] = doc_ref[...].astype(F32)
    for hh in range(2):
        for j in range(3):
            wp_ref[hh, :, HEAD * j : HEAD * j + HEAD] = proj_ref[j, :, HEAD * hh : HEAD * hh + HEAD]
    part[0:128] = nt(x_ref[...], sel_ref[0:RANK]).astype(BF16)
    part[128:160] = nt(sel_ref[RANK:], x_ref[...]).astype(BF16)
    xw[z, x] = wo_ref[...]
    ids[0, :, pl.ds(pl.multiple_of(128 * x, 128), 128)] = ids_ref[...]
    pl.semaphore_wait(barrier, len(everyone))

    slot_pair, slot_rs = links.slots(1), links.slots(1)
    links.start(part, parts.at[0], partner, slot_pair)

    slot_i1 = links.slots(1)
    row_part = pl.ds(pl.multiple_of(128 * x, 128), 128)
    for dx in range(1, NX):
        links.start(ids_ref, ids.at[0, :, row_part], (z, xat(dx), y, c), slot_i1, 2)
    slot_x0 = links.slots(1)
    for hh in range(2):
        links.start(wp_ref.at[hh], wp.at[z, x], (z, 2 * c + hh, y, 1 - x // 2), slot_x0)

    slot_wo, slot_wp = links.slots(4), links.slots(4)
    ringed = pl.ds(pl.multiple_of(2 * other, 2), 2)

    def ring_out(phase):
        for sign in (1, -1):
            block = zat(-sign * 2 * (phase - 1))
            for near in (1, 2):
                far_by = sign * (2 * (phase - 1) + near)
                if far_by != -8:
                    links.start(
                        wo_ref if phase == 1 else xw.at[block, x],
                        xw.at[block, x],
                        (zat(sign * near), x, y, c),
                        slot_wo + phase - 1,
                    )

    def ring_proj(phase):
        for sign in (1, -1):
            block = zat(-sign * 2 * (phase - 1))
            for near in (1, 2):
                far_by = sign * (2 * (phase - 1) + near)
                if far_by != -8:
                    links.start(
                        wp.at[block, ringed],
                        wp.at[block, ringed],
                        (zat(sign * near), x, y, c),
                        slot_wp + phase - 1,
                    )

    def ring_wait(phase):
        links.wait(xw.at[0 : 4 - phase // 4, x], slot_wo + phase - 1, partner)

    def ring_proj_wait(phase):
        links.wait(wp.at[0 : 4 - phase // 4, ringed], slot_wp + phase - 1, partner)

    groups = [[0, -1, 1, -2, 2], [-3, 3, -4, 4], [-5, 5, -6, 6], [-7, 7, 8]]
    slot_near, slot_last = [links.slots(1) for _ in groups], [links.slots(1) for _ in range(2)]

    def spread(g, members):
        for d in members:
            piece = xw.at[zat(-d), x]
            for dx in (1, 3) if g < 2 else (2, 1, 3):
                links.start(piece, piece, (z, xat(dx), y, c), slot_near[g])

    def relay(g):
        links.wait(xw.at[0 : 2 * len(groups[g]), x], slot_near[g], partner)
        middle = (len(groups[g]) + 1) // 2
        for n, d in enumerate(groups[g]):
            toward = 1 if n < middle else -1
            piece = xw.at[zat(-d), xat(-toward)]
            links.start(piece, piece, (z, xat(toward), y, c), slot_last[g])

    def arrived(g):
        if g < 2:
            links.wait(xw.at[0 : len(groups[g]), x], slot_last[g], partner)
        else:
            links.wait(xw.at[0 : 3 * len(groups[g]), x], slot_near[g], partner)

    ring_out(1)
    spread(0, groups[0][:1])
    links.wait(parts.at[0], slot_pair, partner)
    selected = part[...].astype(F32) + parts[0].astype(F32)
    part2[...] = selected.astype(BF16)
    for dy in range(1, NY):
        links.start(part2, parts.at[dy], (z, x, yat(dy), c), slot_rs)
    for n in late:
        loads[n].wait()
    links.wait(ids.at[0, :, 0:384], slot_i1, partner)
    slot_i2 = links.slots(2)
    for dz in range(1, 5):
        links.start(ids.at[0], ids.at[dz], (zat(dz), x, y, c), slot_i2 + min(dz - 1, 1), 6)

    links.wait(wp.at[z, 0:2], slot_x0, partner)
    ring_wait(1)
    ring_out(2)
    spread(0, groups[0][1:])
    ring_proj(1)
    links.wait(parts.at[1:4], slot_rs, partner)
    for k in range(1, NY):
        selected = selected + parts[k].astype(F32)
    values = x_ref[...].astype(F32)
    step = softplus(nn(selected[:RANK].astype(BF16), stepw_ref[...]) + bias_ref[...])
    column = jnp.transpose(jnp.broadcast_to(ids_ref[...], (128, 128)))
    before = pltpu.roll(column, 1, axis=0)
    linked = (column == before) | (iota((128, 128), 0) == 0)
    for k in range(4):
        cols = slice(128 * k, 128 * k + 128)
        dt2[:, cols] = jnp.where(linked, step[:, cols], RESET)
    ss[x] = jnp.sum(dt2[...], axis=0, keepdims=True)
    slot_ss = links.slots(1)
    for dx in range(1, NX):
        links.start(ss.at[x], ss.at[x], (z, xat(dx), y, c), slot_ss, 4)

    driven = (step * values).astype(BF16)
    inputs = jnp.concatenate([selected[RANK : RANK + STATE]] * 16, axis=0)
    for k in range(8):
        token = iota((256, 128), 0) // STATE + k * 16
        spread_in = jnp.where(iota((256, 128), 1) == token, inputs, 0.0).astype(BF16)
        bx[256 * k : 256 * k + 256, :] = nn(spread_in, driven)
    rate = -jnp.exp(a_ref[...]) * LOG2E

    def scan(initial, keep_states):
        def advance(k, h):
            steps = dt2[pl.ds(pl.multiple_of(k * 8, 8), 8), :]
            for j in range(8):
                at = pl.ds(pl.multiple_of(k * 128 + j * 16, 16), 16)
                h = jnp.exp2(rate * steps[j : j + 1, :]) * h + bx[at, :]
                if keep_states:
                    hb[at, :] = h.astype(BF16)
            return h

        return lax.fori_loop(0, 16, advance, initial)

    hs[x] = scan(jnp.zeros((STATE, 512), F32), False).astype(BF16)
    slot_hs = links.slots(1)
    for dx in range(1, NX):
        links.start(hs.at[x], hs.at[x], (z, xat(dx), y, c), slot_hs)
    ring_wait(2)
    ring_out(3)
    spread(1, groups[1])
    relay(0)
    links.wait(ss.at[0:3], slot_ss, partner)
    links.wait(hs.at[0:3], slot_hs, partner)
    links.wait(ids.at[1], slot_i2, partner)
    prior = jnp.where(z == 0, -1.0, ids[1, :, 511:512])
    breaks = []
    for k in range(NX):
        if k:
            prior = ids[0, :, 128 * k - 1 : 128 * k]
        first = ids[0, :, 128 * k : 128 * k + 1]
        breaks.append(jnp.broadcast_to(jnp.where(first == prior, 0.0, RESET), (1, 512)))
    running = jnp.zeros((STATE, 512), F32)
    steps_sum = jnp.zeros((1, 512), F32)
    own_prior, own_steps, own_break = running, steps_sum, steps_sum
    for k in range(NX):
        own_prior = jnp.where(x == k, running, own_prior)
        own_steps = jnp.where(x == k, steps_sum, own_steps)
        own_break = jnp.where(x == k, breaks[k], own_break)
        steps_of = ss[k] + breaks[k]
        running = jnp.exp2(rate * steps_of) * running + hs[k].astype(F32)
        steps_sum = steps_sum + steps_of
    dt2[0:1, :] = dt2[0:1, :] + own_break
    hr[...] = running.astype(BF16)
    sr[...] = steps_sum
    slot_hz, slot_sz = links.slots(1), links.slots(1)
    for dz in range(1, 5):
        links.start(hr, hz.at[dz - 1], (zat(dz), x, y, c), slot_hz)
        links.start(sr, sz.at[dz - 1], (zat(dz), x, y, c), slot_sz, 5)
    ring_wait(3)
    ring_out(4)
    spread(2, groups[2])
    relay(1)
    links.wait(hz, slot_hz, partner)
    links.wait(sz, slot_sz, partner)
    above = jnp.zeros((STATE, 512), F32)
    for dz in range(4, 0, -1):
        joined = jnp.exp2(rate * sz[dz - 1]) * above + hz[dz - 1].astype(F32)
        above = jnp.where(z >= dz, joined, jnp.zeros_like(joined))
    carry = jnp.exp2(rate * own_steps) * above + own_prior
    ring_proj_wait(1)
    ring_proj(2)
    scan(carry, True)
    ring_wait(4)
    spread(3, groups[3])
    pick_out = (lax.rem(iota((STATE, 256), 1), STATE) == iota((STATE, 256), 0)).astype(BF16)
    coefs = lax.dot_general(
        selected[RANK + STATE :].astype(BF16), pick_out, (((0,), (0,)), ((), ())), preferred_element_type=F32
    )
    own_token = iota((16, 256), 1) // STATE == iota((16, 256), 0)

    for k in range(8):
        rows = slice(16 * k, 16 * k + 16)
        coef = jnp.where(own_token, coefs[rows], 0.0).astype(BF16)
        ys[rows, :] = nn(coef, hb[256 * k : 256 * k + 256, :])
    gate = g_ref[...].astype(F32)
    mixed = (ys[...] + skip_ref[...] * values) * (gate / (1.0 + jnp.exp(-gate)))
    gt[...] = mixed.astype(BF16)

    slot_pr = [links.slots(1) for _ in groups]
    slot_r2 = [links.slots(1) for _ in groups]
    half_rows = pl.ds(pl.multiple_of(64 * c, 64), 64)
    their_rows = pl.ds(pl.multiple_of(64 * other, 64), 64)

    def columns(d):
        return pl.ds(pl.multiple_of(128 * zat(-d), 128), 128)

    def weight_of(d):
        return xw[zat(-d)].reshape(128, 512)

    def project_pair(g):
        for d in groups[g]:
            ps[:, columns(d)] = nt(gt[their_rows, :], weight_of(d)).astype(BF16)
        for d in groups[g]:
            piece = ps.at[:, columns(d)]
            links.start(piece, pr.at[:, columns(d)], partner, slot_pr[g])

    def project_own(g):
        for d in groups[g]:
            ow[:, columns(d)] = nt(gt[half_rows, :], weight_of(d))
        width = 128 * len(groups[g])
        links.wait(pr.at[:, 0:width], slot_pr[g], partner)
        for d in groups[g]:
            joined = ow[:, columns(d)] + pr[:, columns(d)].astype(F32)
            ow[:, columns(d)] = joined
            r2s[:, columns(d)] = joined.astype(BF16)
        for d in groups[g]:
            for dy in range(1, NY):
                ty = yat(dy)
                piece = r2s.at[pl.ds(pl.multiple_of(16 * ty, 16), 16), columns(d)]
                links.start(piece, r2.at[dy, :, columns(d)], (z, x, ty, c), slot_r2[g], 1)

    arrived(0)
    project_pair(0)
    arrived(1)
    project_pair(1)
    project_own(0)
    project_own(1)
    ring_proj_wait(2)
    ring_proj(3)
    arrived(2)
    project_pair(2)
    project_own(2)
    arrived(3)
    project_pair(3)
    project_own(3)
    stream = ow[pl.ds(pl.multiple_of(16 * y, 16), 16), :] + res_ref[pl.ds(my_rows, 16), :].astype(F32)
    for g in range(len(groups)):
        width = 128 * len(groups[g])
        links.wait(r2.at[0:3, :, 0:width], slot_r2[g], partner)
    for dy in range(1, NY):
        stream = stream + r2[dy].astype(F32)
    links.wait(ids.at[2:5], slot_i2 + 1, partner)
    stream = stream.astype(BF16).astype(F32)
    normed = stream * lax.rsqrt(jnp.mean(stream * stream, axis=-1, keepdims=True) + EPS) * gain_ref[...]
    normed = normed.astype(BF16)

    na[x, y] = normed[:, :1024]
    nb[x, y] = normed[:, 1024:]
    slot_n1, slot_n2 = links.slots(3), links.slots(3)
    slot_n3, slot_n4 = links.slots(1), links.slots(1)
    for d in range(1, 4):
        links.start(na.at[x, y], na.at[x, y], (z, xat(d), y, c), slot_n1 + d - 1)
        links.start(nb.at[x, y], nb.at[x, y], (z, x, yat(d), c), slot_n2 + d - 1)

    def over_y(k):
        piece = na.at[xat(k), y]
        for d in range(1, 4):
            links.start(piece, piece, (z, x, yat(d), c), slot_n3)

    def over_x(k):
        piece = nb.at[x, yat(k)]
        for d in range(1, 4):
            links.start(piece, piece, (z, xat(d), y, c), slot_n4)

    over_y(0)
    over_x(0)
    ring_proj_wait(3)
    ring_proj(4)

    for k in range(NX):
        qd[k] = jnp.transpose(jnp.broadcast_to(ids[0, :, 128 * k : 128 * k + 128], (128, 128)))
    q_doc = jnp.concatenate([qd[k, half_rows, :] for k in range(NX)], axis=0)
    row_of = iota((256, 128), 0)
    in_row = 128 * (row_of // 64) + 64 * c + lax.rem(row_of, 64)
    for k in (3, 1, 2):
        links.wait(na.at[x, y], slot_n1 + 3 - k, partner)
        over_y(k)
        links.wait(nb.at[x, y], slot_n2 + 3 - k, partner)
        over_x(k)
    ring_proj_wait(4)
    slot_pw = links.slots(1)
    links.start(wp.at[:, ringed], wp.at[:, ringed], partner, slot_pw)

    slot_kz = [None] + [links.slots(4) for _ in range(4)]
    slot_kc = links.slots(5)

    def chunk(d, k, core):
        return kv.at[d, xat(k), core]

    def pass_on(d, k):
        if d < 4:
            links.start(chunk(d, k, c), chunk(d + 1, k, c), (zat(1), x, y, c), slot_kz[d + 1] + k)
        links.start(chunk(d, k, c), chunk(d, k, c), partner, slot_kc + d)

    def forward(d, k):
        links.wait(chunk(d, k, c), slot_kz[d] + k, partner)
        pass_on(d, k)

    links.wait(na.at[0:3], slot_n3, partner)
    links.wait(nb.at[0:3], slot_n4, partner)
    links.wait(wp.at[:, ringed], slot_pw, partner)
    made = nn(na[...].reshape(256, 1024), wp[0:8].reshape(1024, 384))
    made = made + nn(nb[...].reshape(256, 1024), wp[8:16].reshape(1024, 384))
    query = made[:, :HEAD].astype(BF16)
    kv[0, :, c] = made[:, HEAD:].astype(BF16).reshape(4, 64, 256)
    for k in range(4):
        pass_on(0, k)

    def attend(d, carried, blocks):
        top, mass, acc = carried
        links.wait(kv.at[d, :, other], slot_kc + d, partner)
        scores, places = [], []
        for k in blocks:
            place = xat(k)
            piece = nt(query, kv[d, place, :, :, :HEAD].reshape(128, HEAD)) * (HEAD**-0.5 * LOG2E)
            k_doc = jnp.where(z >= d, ids[d, :, pl.ds(pl.multiple_of(128 * place, 128), 128)], -1.0)
            allowed = jnp.broadcast_to(k_doc, (256, 128)) == q_doc
            ahead = iota((256, 128), 1) + 128 * place - in_row
            if d == 0:
                allowed = allowed & (ahead <= 0)
            if d == 4:
                allowed = allowed & (ahead > 0)
            scores.append(jnp.where(allowed, piece, HIDDEN))
            places.append(place)
        highest = scores[0]
        for piece in scores[1:]:
            highest = jnp.maximum(highest, piece)
        new_top = jnp.maximum(top, jnp.max(highest, axis=-1, keepdims=True))
        shrink = jnp.exp2(top - new_top)
        acc = acc * shrink
        added = jnp.zeros((256, 128), F32)
        for place, piece in zip(places, scores):
            probs = jnp.exp2(piece - new_top)
            added = added + probs
            acc = acc + nn(probs.astype(BF16), kv[d, place, :, :, HEAD:].reshape(128, HEAD))
        mass = mass * shrink + jnp.sum(added, axis=-1, keepdims=True)
        return new_top, mass, acc

    carried = (jnp.full((256, 1), HIDDEN, F32), jnp.zeros((256, 1), F32), jnp.zeros((256, HEAD), F32))
    every = (0, 1, 2, 3)
    for d in range(1, 4):
        for k in range(4):
            forward(d, k)
        carried = attend(d - 1, carried, every)
    for k in range(4):
        forward(4, k)
    carried = attend(3, carried, every)
    top, mass, acc = attend(4, carried, every)
    ob[...] = (acc / mass).astype(BF16).reshape(4, 64, HEAD)

    slot_o = links.slots(4)
    mine = slot_o + lax.rem(x, 2) * 2 + c
    cols = pl.ds(pl.multiple_of(128 * lax.rem(x, 2), 128), 128)
    for dx in range(1, NX):
        tx = xat(dx)
        links.start(ob.at[tx], outb.at[half_rows, cols], (z, tx, y, x // 2), mine)
    stays = c == x // 2
    to_partner = links.copy(ob.at[x], outb.at[half_rows, cols], partner, mine, 3)

    @pl.when(stays)
    def _():
        outb[half_rows, cols] = ob[x]

    @pl.when(jnp.logical_not(stays))
    def _():
        to_partner.start()

    for k in range(4):
        from_me = stays & (lax.rem(x, 2) * 2 + c == k)

        @pl.when(jnp.logical_not(from_me))
        def _():
            links.wait(outb.at[half_rows, cols], slot_o + k, partner)

    out_ref[...] = outb[...]

    @pl.when(jnp.logical_not(stays))
    def _():
        to_partner.wait_send()

    for send in range(2):
        assert links.sent[send] % 16384 == 0
        links.drain(send, bx.at[0 : links.sent[send] // 2048], partner)
    links.drain(2, ids.at[0, :, 0:384], partner)
    links.drain(4, ss.at[0:3], partner)
    links.drain(5, sz, partner)
    links.drain(6, ids.at[0:4], partner)
    assert links.recvs <= RECVS, links.recvs


SENDS, RECVS = 7, 68
SEND_MOST = 4 << 20


def body(
    mixer_input, gate_input, document_ids, residual, select_weight, step_weight, step_bias, decay_log, skip_gain,
    out_weight, norm_gain, project_weight,
):
    vmem = pl.BlockSpec(memory_space=pltpu.VMEM)
    hbm = pl.BlockSpec(memory_space=pltpu.HBM)
    operands = (
        mixer_input,
        gate_input,
        document_ids.reshape(1, 128),
        residual,
        select_weight.T,
        step_weight,
        step_bias.reshape(1, 512),
        decay_log.T,
        skip_gain.reshape(1, 512),
        out_weight.T,
        norm_gain.reshape(1, 2048),
        project_weight.transpose(1, 0, 2),
    )
    scratch = [pltpu.VMEM(o.shape, o.dtype) for o in operands]
    scratch += [
        pltpu.VMEM((160, 128), BF16),
        pltpu.VMEM((160, 128), BF16),
        pltpu.VMEM((4, 160, 128), BF16),
        pltpu.VMEM((1, 128), F32),
        pltpu.VMEM((2, 32, 384), BF16),
        pltpu.VMEM((5, 1, 512), F32),
        pltpu.VMEM((128, 512), F32),
        pltpu.VMEM((2048, 512), F32),
        pltpu.VMEM((2048, 512), BF16),
        pltpu.VMEM((4, 16, 512), BF16),
        pltpu.VMEM((4, 1, 512), F32),
        pltpu.VMEM((4, 16, 512), BF16),
        pltpu.VMEM((4, 1, 512), F32),
        pltpu.VMEM((16, 512), BF16),
        pltpu.VMEM((1, 512), F32),
        pltpu.VMEM((16, 4, 32, 512), BF16),
        pltpu.VMEM((16, 4, 32, 384), BF16),
        pltpu.VMEM((128, 512), F32),
        pltpu.VMEM((128, 512), BF16),
        pltpu.VMEM((64, 2048), BF16),
        pltpu.VMEM((64, 2048), BF16),
        pltpu.VMEM((64, 2048), F32),
        pltpu.VMEM((64, 2048), BF16),
        pltpu.VMEM((4, 16, 2048), BF16),
        pltpu.VMEM((4, 4, 16, 1024), BF16),
        pltpu.VMEM((4, 4, 16, 1024), BF16),
        pltpu.VMEM((5, 4, 2, 64, 256), BF16),
        pltpu.VMEM((4, 128, 128), F32),
        pltpu.VMEM((4, 64, 128), BF16),
        pltpu.VMEM((128, 256), BF16),
        pltpu.SemaphoreType.DMA((12,)),
        pltpu.SemaphoreType.DMA((SENDS,)),
        pltpu.SemaphoreType.DMA((RECVS,)),
    ]
    return pl.pallas_call(
        kernel,
        out_shape=jax.ShapeDtypeStruct((128, 256), BF16),
        in_specs=[hbm] * len(operands),
        out_specs=vmem,
        scratch_shapes=scratch,
        compiler_params=pltpu.CompilerParams(collective_id=0, has_side_effects=True, vmem_limit_bytes=67043328),
    )(*operands)


def solution(mesh):
    split = Mesh(mesh.devices.reshape(NZ, NX, NY, NC), ("z", "x", "y", "c"))
    placed = (
        P(SEQ, TP), P(SEQ, TP), P(SEQ), P(SEQ, None), P(TP, None), P(None, TP), P(TP), P(TP, None), P(TP),
        P(TP, SEQ), P(), P(SEQ, None, TP),
    )
    return jax.shard_map(body, mesh=split, in_specs=placed, out_specs=P(SEQ, TP), check_vma=False)
```

time: 88 us -> 81.5 us (0.926)
  Pallas kernels: 84.4 us -> 79.9 us
  local copies, waits for them, and re-layouts: 3.28 us -> 1.47 us
    pallas_call x1, Pallas kernels: 84.4 us -> 79.9 us  [body(): pl.pallas_call(kernel, out_shape=jax.ShapeDtypeStruct((128, 256), BF16),...]
    unnamed x24 -> x1, local copies, waits for them, and re-layouts: 3.13 us -> 1.47 us
where the time goes in v3:
time: 81.5 us; the launch traced here: 81.3 us
  Pallas kernels  79.9 us (98%)
  local copies, waits for them, and re-layouts  1.47 us (2%)
    pallas_call x1, Pallas kernels, body(): pl.pallas_call(kernel, out_shape=jax.ShapeDtypeStruct((128, 256), BF16),...  79.9 us

profile of v3, /device:TPU:1, one launch (start us, length us, event | category | flops | bytes accessed | tf_op | source)
XLA Modules:
  0.0 81.3 jit_solution(362842663103366253)
XLA Ops:
  0.0 79.9 %shard_map.118 = bf16[128,256]{1,0:T(8,128)(2,1)} custom-call(bf16[128,512]{1,0:T(8,128)(2,1)} %refs_0_.1, bf16[128,512]{1,0:T(8,128)(2,1)} %refs_1_.1, s32[1,128]{1,0:T(1,128)} %bitcast.15, bf16[128,2048]{1,0:T(8,128)(2,1)} %refs_3_.1, bf16[160,512]{1,0:T(8,128)(2,1)} %bitcast.8, bf16[128,512]{1,0:T(8,128)(2,1)} %refs_5_.1, f32[1,512]{1,0:T(1,128)} %bitcast.13, ...), custom_call_target="tpu_custom_call" | custom-call | tf_op jit(solution)/shard_map/pallas_call | solution.py:586
  79.9 1.5 %copy.14 = bf16[128,256]{1,0:T(8,128)(2,1)} copy(bf16[128,256]{1,0:T(8,128)(2,1)} %shard_map.118) | data formatting | bytes 131072

commit v4 on v3

--- a/solution.py
+++ b/solution.py
@@ -293,8 +293,8 @@
         links.start(sr, sz.at[dz - 1], (zat(dz), x, y, c), slot_sz, 5)
     ring_wait(3)
     ring_out(4)
+    relay(1)
     spread(2, groups[2])
-    relay(1)
     links.wait(hz, slot_hz, partner)
     links.wait(sz, slot_sz, partner)
     above = jnp.zeros((STATE, 512), F32)
@@ -360,11 +360,11 @@
     project_pair(1)
     project_own(0)
     project_own(1)
-    ring_proj_wait(2)
-    ring_proj(3)
     arrived(2)
     project_pair(2)
     project_own(2)
+    ring_proj_wait(2)
+    ring_proj(3)
     arrived(3)
     project_pair(3)
     project_own(3)
@@ -473,13 +473,17 @@
 
     carried = (jnp.full((256, 1), HIDDEN, F32), jnp.zeros((256, 1), F32), jnp.zeros((256, HEAD), F32))
     every = (0, 1, 2, 3)
+    carried = attend(0, carried, every)
     for d in range(1, 4):
         for k in range(4):
             forward(d, k)
-        carried = attend(d - 1, carried, every)
-    for k in range(4):
-        forward(4, k)
+        if d > 1:
+            carried = attend(d - 1, carried, every)
+    forward(4, 0)
+    forward(4, 1)
     carried = attend(3, carried, every)
+    forward(4, 2)
+    forward(4, 3)
     top, mass, acc = attend(4, carried, every)
     ob[...] = (acc / mass).astype(BF16).reshape(4, 64, HEAD)
 
@@ -589,8 +593,8 @@
         in_specs=[hbm] * len(operands),
         out_specs=vmem,
         scratch_shapes=scratch,
-        compiler_params=pltpu.CompilerParams(collective_id=0, has_side_effects=True, vmem_limit_bytes=67043328),
-    )(*operands)
+        compiler_params=pltpu.CompilerParams(collective_id=0, has_side_effects=True, vmem_limit_bytes=48 << 20),
+    )(*[pltpu.with_memory_space_constraint(o, pltpu.HBM) for o in operands])
 
 
 def solution(mesh):

time: 81.5 us -> 78.8 us (0.967)
  Pallas kernels: 79.9 us -> 78 us
  local copies, waits for them, and re-layouts: 1.47 us -> 0.63 us
    pallas_call x1, Pallas kernels: 79.9 us -> 78 us  [body(): pl.pallas_call(kernel, out_shape=jax.ShapeDtypeStruct((128, 256), BF16),...]
    unnamed x1, local copies, waits for them, and re-layouts: 1.47 us -> 0.63 us
where the time goes in v4:
time: 78.8 us; the launch traced here: 78.7 us
  Pallas kernels  78 us (99%)
    pallas_call x1, Pallas kernels, body(): pl.pallas_call(kernel, out_shape=jax.ShapeDtypeStruct((128, 256), BF16),...  78 us

profile of v4, /device:TPU:1, one launch (start us, length us, event | category | flops | bytes accessed | tf_op | source)
XLA Modules:
  0.0 78.7 jit_solution(5562700057650134312)
XLA Ops:
  0.0 78.0 %shard_map.118 = bf16[128,256]{1,0:T(8,128)(2,1)S(1)} custom-call(bf16[128,512]{1,0:T(8,128)(2,1)} %refs_0_.1, bf16[128,512]{1,0:T(8,128)(2,1)} %refs_1_.1, s32[1,128]{1,0:T(1,128)} %bitcast.15, bf16[128,2048]{1,0:T(8,128)(2,1)} %refs_3_.1, bf16[160,512]{1,0:T(8,128)(2,1)} %bitcast.8, bf16[128,512]{1,0:T(8,128)(2,1)} %refs_5_.1, f32[1,512]{1,0:T(1,128)} %bitcast.13, ...), custom_call_target="tpu_custom_call" | custom-call | tf_op jit(solution)/shard_map/pallas_call | solution.py:590
  78.0 0.6 copy.14

commit v5 on v4

--- a/solution.py
+++ b/solution.py
@@ -85,7 +85,7 @@
     staged, refs = refs[:12], refs[12:]
     x_ref, g_ref, doc_ref, res_ref, sel_ref, stepw_ref, bias_ref, a_ref, skip_ref, wo_ref, gain_ref, proj_ref = staged
     (
-        part, part2, parts, ids_ref, wp_ref, ids, dt2, bx, hb, hs, ss, hz, sz, hr, sr, xw, wp, ys, gt, ps, pr, ow, r2s, r2, na, nb,
+        part, part2, parts, ids_ref, wp_ref, ids, dt2, bx, hb, hs, ss, hz, sz, hr, sr, xw, wp, ys, gt, ps, pr, pf, r2s, r2, p3, f3, r3, na, nb,
         kv, qd, ob, outb, local_sem, send_sem, recv_sem,
     ) = refs
     z, x, y, c = (lax.axis_index(n) for n in ("z", "x", "y", "c"))
@@ -112,6 +112,11 @@
         pl.semaphore_signal(barrier, inc=1, device_id=device, device_id_type=MESH)
 
     links = Links(send_sem, recv_sem)
+    groups = [[0, -1, 1, -2, 2], [-3, 3, -4, 4], [-5, 5, -6, 6], [-7, 7, 8]]
+
+    def columns(d):
+        return pl.ds(pl.multiple_of(128 * zat(-d), 128), 128)
+
     loads = [pltpu.make_async_copy(src, dst, local_sem.at[n]) for n, (src, dst) in enumerate(zip(homes, staged))]
     early = (0, 4, 2, 9, 11)
     late = (5, 6, 7, 8, 1, 3, 10)
@@ -130,6 +135,8 @@
     part[128:160] = nt(sel_ref[RANK:], x_ref[...]).astype(BF16)
     xw[z, x] = wo_ref[...]
     ids[0, :, pl.ds(pl.multiple_of(128 * x, 128), 128)] = ids_ref[...]
+    for d in groups[3]:
+        r2[:, :, columns(d)] = jnp.zeros((4, 16, 128), BF16)
     pl.semaphore_wait(barrier, len(everyone))
 
     slot_pair, slot_rs = links.slots(1), links.slots(1)
@@ -143,20 +150,19 @@
     for hh in range(2):
         links.start(wp_ref.at[hh], wp.at[z, x], (z, 2 * c + hh, y, 1 - x // 2), slot_x0)
 
-    slot_wo, slot_wp = links.slots(4), links.slots(4)
+    slot_wo, slot_wp = links.slots(8), links.slots(4)
     ringed = pl.ds(pl.multiple_of(2 * other, 2), 2)
 
     def ring_out(phase):
-        for sign in (1, -1):
-            block = zat(-sign * 2 * (phase - 1))
-            for near in (1, 2):
-                far_by = sign * (2 * (phase - 1) + near)
-                if far_by != -8:
+        for near in (2, 1):
+            for sign in (1, -1):
+                block = zat(-sign * 2 * (phase - 1))
+                if sign * (2 * (phase - 1) + near) != -8:
                     links.start(
                         wo_ref if phase == 1 else xw.at[block, x],
                         xw.at[block, x],
                         (zat(sign * near), x, y, c),
-                        slot_wo + phase - 1,
+                        slot_wo + 2 * phase - near,
                     )
 
     def ring_proj(phase):
@@ -172,13 +178,15 @@
                         slot_wp + phase - 1,
                     )
 
-    def ring_wait(phase):
-        links.wait(xw.at[0 : 4 - phase // 4, x], slot_wo + phase - 1, partner)
+    def ring_far(phase):
+        links.wait(xw.at[0 : 2 - phase // 4, x], slot_wo + 2 * phase - 2, partner)
+
+    def ring_near(phase):
+        links.wait(xw.at[0:2, x], slot_wo + 2 * phase - 1, partner)
 
     def ring_proj_wait(phase):
         links.wait(wp.at[0 : 4 - phase // 4, ringed], slot_wp + phase - 1, partner)
 
-    groups = [[0, -1, 1, -2, 2], [-3, 3, -4, 4], [-5, 5, -6, 6], [-7, 7, 8]]
     slot_near, slot_last = [links.slots(1) for _ in groups], [links.slots(1) for _ in range(2)]
 
     def spread(g, members):
@@ -215,10 +223,11 @@
     for dz in range(1, 5):
         links.start(ids.at[0], ids.at[dz], (zat(dz), x, y, c), slot_i2 + min(dz - 1, 1), 6)
 
+    ring_far(1)
+    ring_out(2)
+    ring_near(1)
+    spread(0, groups[0][1:])
     links.wait(wp.at[z, 0:2], slot_x0, partner)
-    ring_wait(1)
-    ring_out(2)
-    spread(0, groups[0][1:])
     ring_proj(1)
     links.wait(parts.at[1:4], slot_rs, partner)
     for k in range(1, NY):
@@ -260,8 +269,9 @@
     slot_hs = links.slots(1)
     for dx in range(1, NX):
         links.start(hs.at[x], hs.at[x], (z, xat(dx), y, c), slot_hs)
-    ring_wait(2)
+    ring_far(2)
     ring_out(3)
+    ring_near(2)
     spread(1, groups[1])
     relay(0)
     links.wait(ss.at[0:3], slot_ss, partner)
@@ -291,10 +301,14 @@
     for dz in range(1, 5):
         links.start(hr, hz.at[dz - 1], (zat(dz), x, y, c), slot_hz)
         links.start(sr, sz.at[dz - 1], (zat(dz), x, y, c), slot_sz, 5)
-    ring_wait(3)
+    ring_far(3)
     ring_out(4)
+    ring_near(3)
     relay(1)
     spread(2, groups[2])
+    ring_far(4)
+    ring_near(4)
+    spread(3, groups[3])
     links.wait(hz, slot_hz, partner)
     links.wait(sz, slot_sz, partner)
     above = jnp.zeros((STATE, 512), F32)
@@ -305,8 +319,6 @@
     ring_proj_wait(1)
     ring_proj(2)
     scan(carry, True)
-    ring_wait(4)
-    spread(3, groups[3])
     pick_out = (lax.rem(iota((STATE, 256), 1), STATE) == iota((STATE, 256), 0)).astype(BF16)
     coefs = lax.dot_general(
         selected[RANK + STATE :].astype(BF16), pick_out, (((0,), (0,)), ((), ())), preferred_element_type=F32
@@ -326,52 +338,62 @@
     half_rows = pl.ds(pl.multiple_of(64 * c, 64), 64)
     their_rows = pl.ds(pl.multiple_of(64 * other, 64), 64)
 
-    def columns(d):
-        return pl.ds(pl.multiple_of(128 * zat(-d), 128), 128)
-
     def weight_of(d):
         return xw[zat(-d)].reshape(128, 512)
 
-    def project_pair(g):
+    def project(g):
         for d in groups[g]:
-            ps[:, columns(d)] = nt(gt[their_rows, :], weight_of(d)).astype(BF16)
+            pf[:, columns(d)] = nt(gt[...], weight_of(d))
         for d in groups[g]:
-            piece = ps.at[:, columns(d)]
-            links.start(piece, pr.at[:, columns(d)], partner, slot_pr[g])
-
-    def project_own(g):
-        for d in groups[g]:
-            ow[:, columns(d)] = nt(gt[half_rows, :], weight_of(d))
+            ps[:, columns(d)] = pf[their_rows, columns(d)].astype(BF16)
+            links.start(ps.at[:, columns(d)], pr.at[:, columns(d)], partner, slot_pr[g])
+
+    def finish(g):
         width = 128 * len(groups[g])
         links.wait(pr.at[:, 0:width], slot_pr[g], partner)
         for d in groups[g]:
-            joined = ow[:, columns(d)] + pr[:, columns(d)].astype(F32)
-            ow[:, columns(d)] = joined
+            joined = pf[half_rows, columns(d)] + pr[:, columns(d)].astype(F32)
+            pf[half_rows, columns(d)] = joined
             r2s[:, columns(d)] = joined.astype(BF16)
         for d in groups[g]:
             for dy in range(1, NY):
                 ty = yat(dy)
                 piece = r2s.at[pl.ds(pl.multiple_of(16 * ty, 16), 16), columns(d)]
-                links.start(piece, r2.at[dy, :, columns(d)], (z, x, ty, c), slot_r2[g], 1)
+                links.start(piece, r2.at[dy, :, columns(d)], (z, x, ty, c), slot_r2[g], 8)
 
     arrived(0)
-    project_pair(0)
+    project(0)
     arrived(1)
-    project_pair(1)
-    project_own(0)
-    project_own(1)
+    project(1)
+    finish(0)
     arrived(2)
-    project_pair(2)
-    project_own(2)
+    project(2)
+    finish(1)
     ring_proj_wait(2)
     ring_proj(3)
+    finish(2)
     arrived(3)
-    project_pair(3)
-    project_own(3)
-    stream = ow[pl.ds(pl.multiple_of(16 * y, 16), 16), :] + res_ref[pl.ds(my_rows, 16), :].astype(F32)
-    for g in range(len(groups)):
+    slot_r3 = links.slots(1)
+    for j, d in enumerate(groups[3]):
+        product = nt(gt[...], weight_of(d))
+        f3[:, 128 * j : 128 * j + 128] = product
+        p3[:, 128 * j : 128 * j + 128] = product.astype(BF16)
+    for dy in range(NY):
+        for dc in range(NC):
+            if dy or dc:
+                ty, tc = yat(dy), cat(dc)
+                rows = pl.ds(pl.multiple_of(64 * tc + 16 * ty, 16), 16)
+                links.start(p3.at[rows], r3.at[dy * 2 + dc], (z, x, ty, tc), slot_r3, 7)
+    for g in range(3):
         width = 128 * len(groups[g])
         links.wait(r2.at[0:3, :, 0:width], slot_r2[g], partner)
+    links.wait(r3.at[1:8], slot_r3, partner)
+    straight = f3[pl.ds(my_rows, 16), :]
+    for k in range(1, 8):
+        straight = straight + r3[k].astype(F32)
+    for j, d in enumerate(groups[3]):
+        pf[pl.ds(my_rows, 16), columns(d)] = straight[:, 128 * j : 128 * j + 128]
+    stream = pf[pl.ds(my_rows, 16), :] + res_ref[pl.ds(my_rows, 16), :].astype(F32)
     for dy in range(1, NY):
         stream = stream + r2[dy].astype(F32)
     links.wait(ids.at[2:5], slot_i2 + 1, partner)
@@ -441,50 +463,50 @@
     for k in range(4):
         pass_on(0, k)
 
-    def attend(d, carried, blocks):
+    def attend(d, half, carried):
         top, mass, acc = carried
-        links.wait(kv.at[d, :, other], slot_kc + d, partner)
-        scores, places = [], []
-        for k in blocks:
-            place = xat(k)
-            piece = nt(query, kv[d, place, :, :, :HEAD].reshape(128, HEAD)) * (HEAD**-0.5 * LOG2E)
-            k_doc = jnp.where(z >= d, ids[d, :, pl.ds(pl.multiple_of(128 * place, 128), 128)], -1.0)
-            allowed = jnp.broadcast_to(k_doc, (256, 128)) == q_doc
-            ahead = iota((256, 128), 1) + 128 * place - in_row
+        rows = slice(128 * half, 128 * half + 128)
+        scores = []
+        for k in range(NX):
+            piece = nt(query[rows], kv[d, k, :, :, :HEAD].reshape(128, HEAD)) * (HEAD**-0.5 * LOG2E)
+            k_doc = jnp.where(z >= d, ids[d, :, 128 * k : 128 * k + 128], -1.0)
+            allowed = jnp.broadcast_to(k_doc, (128, 128)) == q_doc[rows]
+            ahead = iota((128, 128), 1) + 128 * k - in_row[rows]
             if d == 0:
                 allowed = allowed & (ahead <= 0)
             if d == 4:
                 allowed = allowed & (ahead > 0)
             scores.append(jnp.where(allowed, piece, HIDDEN))
-            places.append(place)
-        highest = scores[0]
-        for piece in scores[1:]:
-            highest = jnp.maximum(highest, piece)
+        highest = jnp.maximum(jnp.maximum(scores[0], scores[1]), jnp.maximum(scores[2], scores[3]))
         new_top = jnp.maximum(top, jnp.max(highest, axis=-1, keepdims=True))
         shrink = jnp.exp2(top - new_top)
-        acc = acc * shrink
-        added = jnp.zeros((256, 128), F32)
-        for place, piece in zip(places, scores):
-            probs = jnp.exp2(piece - new_top)
-            added = added + probs
-            acc = acc + nn(probs.astype(BF16), kv[d, place, :, :, HEAD:].reshape(128, HEAD))
+        probs = [jnp.exp2(piece - new_top) for piece in scores]
+        added = (probs[0] + probs[1]) + (probs[2] + probs[3])
         mass = mass * shrink + jnp.sum(added, axis=-1, keepdims=True)
+        joined = jnp.concatenate([p.astype(BF16) for p in probs], axis=1)
+        acc = acc * shrink + nn(joined, kv[d, :, :, :, HEAD:].reshape(512, HEAD))
         return new_top, mass, acc
 
-    carried = (jnp.full((256, 1), HIDDEN, F32), jnp.zeros((256, 1), F32), jnp.zeros((256, HEAD), F32))
-    every = (0, 1, 2, 3)
-    carried = attend(0, carried, every)
-    for d in range(1, 4):
-        for k in range(4):
-            forward(d, k)
-        if d > 1:
-            carried = attend(d - 1, carried, every)
-    forward(4, 0)
-    forward(4, 1)
-    carried = attend(3, carried, every)
-    forward(4, 2)
-    forward(4, 3)
-    top, mass, acc = attend(4, carried, every)
+    def shared(d):
+        links.wait(kv.at[d, :, other], slot_kc + d, partner)
+
+    start = (jnp.full((128, 1), HIDDEN, F32), jnp.zeros((128, 1), F32), jnp.zeros((128, HEAD), F32))
+    shared(0)
+    first, second = attend(0, 0, start), attend(0, 1, start)
+    for k in range(4):
+        forward(1, k)
+    for d in range(2, 5):
+        forward(d, 0)
+        forward(d, 1)
+        shared(d - 1)
+        first = attend(d - 1, 0, first)
+        forward(d, 2)
+        forward(d, 3)
+        second = attend(d - 1, 1, second)
+    shared(4)
+    first, second = attend(4, 0, first), attend(4, 1, second)
+    mass = jnp.concatenate([first[1], second[1]], axis=0)
+    acc = jnp.concatenate([first[2], second[2]], axis=0)
     ob[...] = (acc / mass).astype(BF16).reshape(4, 64, HEAD)
 
     slot_o = links.slots(4)
@@ -522,12 +544,14 @@
         links.drain(send, bx.at[0 : links.sent[send] // 2048], partner)
     links.drain(2, ids.at[0, :, 0:384], partner)
     links.drain(4, ss.at[0:3], partner)
+    links.drain(7, r3.at[1:8], partner)
+    links.drain(8, r2.at[0:3, :, 0:1664], partner)
     links.drain(5, sz, partner)
     links.drain(6, ids.at[0:4], partner)
     assert links.recvs <= RECVS, links.recvs
 
 
-SENDS, RECVS = 7, 68
+SENDS, RECVS = 9, 72
 SEND_MOST = 4 << 20
 
 
@@ -574,9 +598,12 @@
         pltpu.VMEM((128, 512), BF16),
         pltpu.VMEM((64, 2048), BF16),
         pltpu.VMEM((64, 2048), BF16),
-        pltpu.VMEM((64, 2048), F32),
+        pltpu.VMEM((128, 2048), F32),
         pltpu.VMEM((64, 2048), BF16),
         pltpu.VMEM((4, 16, 2048), BF16),
+        pltpu.VMEM((128, 384), BF16),
+        pltpu.VMEM((128, 384), F32),
+        pltpu.VMEM((8, 16, 384), BF16),
         pltpu.VMEM((4, 4, 16, 1024), BF16),
         pltpu.VMEM((4, 4, 16, 1024), BF16),
         pltpu.VMEM((5, 4, 2, 64, 256), BF16),

time: 78.8 us -> 77.8 us (0.987)
  Pallas kernels: 78 us -> 77 us
    pallas_call x1, Pallas kernels: 78 us -> 77 us  [body(): pl.pallas_call(kernel, out_shape=jax.ShapeDtypeStruct((128, 256), BF16),...]
where the time goes in v5:
time: 77.8 us; the launch traced here: 77.7 us
  Pallas kernels  77 us (99%)
    pallas_call x1, Pallas kernels, body(): pl.pallas_call(kernel, out_shape=jax.ShapeDtypeStruct((128, 256), BF16),...  77 us

profile of v5, /device:TPU:1, one launch (start us, length us, event | category | flops | bytes accessed | tf_op | source)
XLA Modules:
  0.0 77.7 jit_solution(6454777419120099917)
XLA Ops:
  0.0 77.0 %shard_map.118 = bf16[128,256]{1,0:T(8,128)(2,1)S(1)} custom-call(bf16[128,512]{1,0:T(8,128)(2,1)} %refs_0_.1, bf16[128,512]{1,0:T(8,128)(2,1)} %refs_1_.1, s32[1,128]{1,0:T(1,128)} %bitcast.15, bf16[128,2048]{1,0:T(8,128)(2,1)} %refs_3_.1, bf16[160,512]{1,0:T(8,128)(2,1)} %bitcast.8, bf16[128,512]{1,0:T(8,128)(2,1)} %refs_5_.1, f32[1,512]{1,0:T(1,128)} %bitcast.13, ...), custom_call_target="tpu_custom_call" | custom-call | tf_op jit(solution)/shard_map/pallas_call | solution.py:617
  77.0 0.6 copy.14

commit v6 on v5

--- a/solution.py
+++ b/solution.py
@@ -85,7 +85,7 @@
     staged, refs = refs[:12], refs[12:]
     x_ref, g_ref, doc_ref, res_ref, sel_ref, stepw_ref, bias_ref, a_ref, skip_ref, wo_ref, gain_ref, proj_ref = staged
     (
-        part, part2, parts, ids_ref, wp_ref, ids, dt2, bx, hb, hs, ss, hz, sz, hr, sr, xw, wp, ys, gt, ps, pr, pf, r2s, r2, p3, f3, r3, na, nb,
+        part, part2, parts, ids_ref, wp_ref, ids, dt2, bx, hb, hs, ss, hz, sz, hr, sr, xw, wp, ys, gt, ps, pr, pf, r2s, r2, st, p3, f3, r3, na, nb,
         kv, qd, ob, outb, local_sem, send_sem, recv_sem,
     ) = refs
     z, x, y, c = (lax.axis_index(n) for n in ("z", "x", "y", "c"))
@@ -135,8 +135,7 @@
     part[128:160] = nt(sel_ref[RANK:], x_ref[...]).astype(BF16)
     xw[z, x] = wo_ref[...]
     ids[0, :, pl.ds(pl.multiple_of(128 * x, 128), 128)] = ids_ref[...]
-    for d in groups[3]:
-        r2[:, :, columns(d)] = jnp.zeros((4, 16, 128), BF16)
+    r2[:, :, 1664:] = jnp.zeros((4, 16, 384), BF16)
     pl.semaphore_wait(barrier, len(everyone))
 
     slot_pair, slot_rs = links.slots(1), links.slots(1)
@@ -341,25 +340,27 @@
     def weight_of(d):
         return xw[zat(-d)].reshape(128, 512)
 
+    starts = [128 * sum(len(before) for before in groups[:g]) for g in range(len(groups))]
+
+    def span(g):
+        return slice(starts[g], starts[g] + 128 * len(groups[g]))
+
     def project(g):
-        for d in groups[g]:
-            pf[:, columns(d)] = nt(gt[...], weight_of(d))
-        for d in groups[g]:
-            ps[:, columns(d)] = pf[their_rows, columns(d)].astype(BF16)
-            links.start(ps.at[:, columns(d)], pr.at[:, columns(d)], partner, slot_pr[g])
+        for n, d in enumerate(groups[g]):
+            at = starts[g] + 128 * n
+            pf[:, at : at + 128] = nt(gt[...], weight_of(d))
+        ps[:, span(g)] = pf[their_rows, span(g)].astype(BF16)
+        links.start(ps.at[:, span(g)], pr.at[:, span(g)], partner, slot_pr[g])
 
     def finish(g):
-        width = 128 * len(groups[g])
-        links.wait(pr.at[:, 0:width], slot_pr[g], partner)
-        for d in groups[g]:
-            joined = pf[half_rows, columns(d)] + pr[:, columns(d)].astype(F32)
-            pf[half_rows, columns(d)] = joined
-            r2s[:, columns(d)] = joined.astype(BF16)
-        for d in groups[g]:
-            for dy in range(1, NY):
-                ty = yat(dy)
-                piece = r2s.at[pl.ds(pl.multiple_of(16 * ty, 16), 16), columns(d)]
-                links.start(piece, r2.at[dy, :, columns(d)], (z, x, ty, c), slot_r2[g], 8)
+        links.wait(pr.at[:, span(g)], slot_pr[g], partner)
+        joined = pf[half_rows, span(g)] + pr[:, span(g)].astype(F32)
+        pf[half_rows, span(g)] = joined
+        r2s[:, span(g)] = joined.astype(BF16)
+        for dy in range(1, NY):
+            ty = yat(dy)
+            piece = r2s.at[pl.ds(pl.multiple_of(16 * ty, 16), 16), span(g)]
+            links.start(piece, r2.at[dy, :, span(g)], (z, x, ty, c), slot_r2[g], 8)
 
     arrived(0)
     project(0)
@@ -385,17 +386,18 @@
                 rows = pl.ds(pl.multiple_of(64 * tc + 16 * ty, 16), 16)
                 links.start(p3.at[rows], r3.at[dy * 2 + dc], (z, x, ty, tc), slot_r3, 7)
     for g in range(3):
-        width = 128 * len(groups[g])
-        links.wait(r2.at[0:3, :, 0:width], slot_r2[g], partner)
+        links.wait(r2.at[0:3, :, span(g)], slot_r2[g], partner)
     links.wait(r3.at[1:8], slot_r3, partner)
     straight = f3[pl.ds(my_rows, 16), :]
     for k in range(1, 8):
         straight = straight + r3[k].astype(F32)
-    for j, d in enumerate(groups[3]):
-        pf[pl.ds(my_rows, 16), columns(d)] = straight[:, 128 * j : 128 * j + 128]
-    stream = pf[pl.ds(my_rows, 16), :] + res_ref[pl.ds(my_rows, 16), :].astype(F32)
+    pf[pl.ds(my_rows, 16), span(3)] = straight
+    stream = pf[pl.ds(my_rows, 16), :]
     for dy in range(1, NY):
         stream = stream + r2[dy].astype(F32)
+    for n, d in enumerate(sum(groups, [])):
+        st[:, columns(d)] = stream[:, 128 * n : 128 * n + 128]
+    stream = st[...] + res_ref[pl.ds(my_rows, 16), :].astype(F32)
     links.wait(ids.at[2:5], slot_i2 + 1, partner)
     stream = stream.astype(BF16).astype(F32)
     normed = stream * lax.rsqrt(jnp.mean(stream * stream, axis=-1, keepdims=True) + EPS) * gain_ref[...]
@@ -601,6 +603,7 @@
         pltpu.VMEM((128, 2048), F32),
         pltpu.VMEM((64, 2048), BF16),
         pltpu.VMEM((4, 16, 2048), BF16),
+        pltpu.VMEM((16, 2048), F32),
         pltpu.VMEM((128, 384), BF16),
         pltpu.VMEM((128, 384), F32),
         pltpu.VMEM((8, 16, 384), BF16),

time: 77.8 us -> 77.8 us (level)
  no operation moved by 1% of the time
where the time goes in v6:
time: 77.8 us; the launch traced here: 77.7 us
  Pallas kernels  77 us (99%)
    pallas_call x1, Pallas kernels, body(): pl.pallas_call(kernel, out_shape=jax.ShapeDtypeStruct((128, 256), BF16),...  77 us

profile of v6, /device:TPU:1, one launch (start us, length us, event | category | flops | bytes accessed | tf_op | source)
XLA Modules:
  0.0 77.7 jit_solution(12143801915165374298)
XLA Ops:
  0.0 77.0 %shard_map.118 = bf16[128,256]{1,0:T(8,128)(2,1)S(1)} custom-call(bf16[128,512]{1,0:T(8,128)(2,1)} %refs_0_.1, bf16[128,512]{1,0:T(8,128)(2,1)} %refs_1_.1, s32[1,128]{1,0:T(1,128)} %bitcast.15, bf16[128,2048]{1,0:T(8,128)(2,1)} %refs_3_.1, bf16[160,512]{1,0:T(8,128)(2,1)} %bitcast.8, bf16[128,512]{1,0:T(8,128)(2,1)} %refs_5_.1, f32[1,512]{1,0:T(1,128)} %bitcast.13, ...), custom_call_target="tpu_custom_call" | custom-call | tf_op jit(solution)/shard_map/pallas_call | solution.py:620
  77.0 0.6 copy.14

commit v7 on v6

--- a/solution.py
+++ b/solution.py
@@ -370,9 +370,9 @@
     arrived(2)
     project(2)
     finish(1)
+    finish(2)
     ring_proj_wait(2)
     ring_proj(3)
-    finish(2)
     arrived(3)
     slot_r3 = links.slots(1)
     for j, d in enumerate(groups[3]):

time: 77.8 us -> 77.8 us (level)
  no operation moved by 1% of the time
where the time goes in v7:
time: 77.8 us; the launch traced here: 77.7 us
  Pallas kernels  77 us (99%)
    pallas_call x1, Pallas kernels, body(): pl.pallas_call(kernel, out_shape=jax.ShapeDtypeStruct((128, 256), BF16),...  77 us

profile of v7, /device:TPU:1, one launch (start us, length us, event | category | flops | bytes accessed | tf_op | source)
XLA Modules:
  0.0 77.7 jit_solution(218605783595639180)
XLA Ops:
  0.0 77.0 %shard_map.118 = bf16[128,256]{1,0:T(8,128)(2,1)S(1)} custom-call(bf16[128,512]{1,0:T(8,128)(2,1)} %refs_0_.1, bf16[128,512]{1,0:T(8,128)(2,1)} %refs_1_.1, s32[1,128]{1,0:T(1,128)} %bitcast.15, bf16[128,2048]{1,0:T(8,128)(2,1)} %refs_3_.1, bf16[160,512]{1,0:T(8,128)(2,1)} %bitcast.8, bf16[128,512]{1,0:T(8,128)(2,1)} %refs_5_.1, f32[1,512]{1,0:T(1,128)} %bitcast.13, ...), custom_call_target="tpu_custom_call" | custom-call | tf_op jit(solution)/shard_map/pallas_call | solution.py:620
  77.0 0.6 copy.14
